TPU v7x, 32 devices: a whole 2x2x4 slice. The times are simulated.
32 devices in a mesh: chain: 8 (over y, x, core), lane: 4 (over z).
Axes of the slice: x: 2, y: 2, z: 4, core: 2. Of those that a mesh axis runs over, the one named last changes fastest.
Arguments:
- fiedler: float32 [16, 96, 128, 128], P(None, 'chain', 'lane'), may hold values from -6 to 6
- side_labels: int32 [96, 128, 128], P('chain', 'lane'), may hold values from 0 to 1, as said below
Outputs:
- squared_image: float32 [16, 120, 128, 128], P(None, 'chain', 'lane')
- gram_blocks: float32 [2, 16, 16], replicated
Inputs may be any that keep to these rules, and one draw needn't show every extreme that they name: `side_labels`: along every line of the first dimension (fixed second and third index) the vertices of side 0 form one run of planes [a, b) with 18 <= a <= 30 and 66 <= b <= 78; all other vertices are of side 1.
All inputs are finite; a program needn't handle non-finite values.
Results may differ from a plain program's by a relative error of at most 0.0001.
Values sent between devices are 32-bit elements; how exact they have to be, the bound alone decides.
A program may use at most 128 MiB of HBM per device.

v0:
```python
import functools

import jax
import jax.numpy as jnp
import numpy as np
from jax import lax
from jax.experimental import pallas as pl
from jax.experimental.pallas import tpu as pltpu
from jax.sharding import PartitionSpec as P

REACH = 2


def band_plan(chain_count, plane_count):
    half_count = chain_count // 2
    band_planes = plane_count + plane_count // 4
    total_planes = plane_count * chain_count
    margin_planes = (band_planes - plane_count) * half_count // 2
    own_slot = np.zeros(chain_count, np.int32)
    bounds = np.zeros((2, chain_count), np.int32)
    sides = np.zeros(chain_count, np.int32)
    transfers = []
    for target in range(chain_count):
        relative = (target - chain_count // 4) % chain_count
        side = relative // half_count
        within = relative % half_count
        first = total_planes // 4 - margin_planes + side * (total_planes // 2) + within * band_planes - REACH
        slot = (target * plane_count - first + total_planes // 2) % total_planes - total_planes // 2
        low = REACH if within == 0 else 0
        high = band_planes + (REACH if within == half_count - 1 else 2 * REACH)
        own_slot[target], sides[target] = slot, side
        bounds[:, target] = low, high
        below, above = max(0, slot - low), max(0, high - slot - plane_count)
        assert below <= plane_count and above <= plane_count
        if below:
            transfers.append((below, (target - 1) % chain_count, target, 1))
        if above:
            transfers.append((above, (target + 1) % chain_count, target, 2))
    groups = []
    for count, source, target, way in sorted(transfers, reverse=True):
        for group in groups:
            if group["count"] == count and source not in group["sources"] and target not in group["targets"]:
                break
        else:
            group = dict(count=count, sources=[], targets=[], start=np.zeros(chain_count, np.int32),
                         arrives=np.full(chain_count, -1, np.int32))
            groups.append(group)
        group["sources"].append(source)
        group["targets"].append(target)
        group["start"][source] = plane_count - count if way == 1 else 0
        group["arrives"][target] = plane_count + own_slot[target] + (-count if way == 1 else plane_count)
    return band_planes, own_slot, bounds, sides, groups


def two_sided(field):
    return (
        pltpu.roll(field, 1, 0) + pltpu.roll(field, field.shape[0] - 1, 0)
        + pltpu.roll(field, 1, 1) + pltpu.roll(field, field.shape[1] - 1, 1)
    )


def laplace_kernel(counts, planes, lines, band, vectors, slots, table, *refs):
    groups = len(counts)
    own, own_marks, edge, edge_marks = refs[:4]
    got = refs[4 : 4 + 4 * groups]
    image, gram, field, mark, scale, degree, once, kept = refs[4 + 4 * groups :]
    k = pl.program_id(0)
    window = band + 2 * REACH

    def place(dest, start, count, body, border):
        dest[pl.ds(start, count), 0:lines, :] = body
        dest[pl.ds(start, count), lines : lines + REACH, :] = border[:, 0:REACH]
        dest[pl.ds(start, count), lines + 8 - REACH : lines + 8, :] = border[:, REACH:]

    def gather(dest, body, border, which):
        place(dest, planes + table[0], planes, body, border)
        for g in range(groups):
            start = table[4 + g]

            @pl.when(start >= 0)
            def _():
                place(dest, start, counts[g], got[4 * g + which][0], got[4 * g + 2 + which][0])

    @pl.when(k == 0)
    def _():
        mark[...] = jnp.full(mark.shape, -1.0, jnp.float32)
        gather(mark, own_marks[...].astype(jnp.float32), edge_marks[0], 1)
        side = table[3].astype(jnp.float32)
        for s in range(window):
            inside = (s >= table[1]) & (s < table[2])
            here = jnp.where(inside, side, jnp.float32(-2.0))
            mark[planes + s] = (mark[planes + s] == here).astype(jnp.float32)
        for s in range(1, window - 1):
            at = planes + s
            total = mark[at - 1] + mark[at + 1] + two_sided(mark[at])
            scale[s] = mark[at] / 6.0
            degree[s] = mark[at] * total / 6.0

    gather(field, own[0], edge[0], 0)

    def moved(s):
        return jnp.where(mark[planes + s] > 0.5, field[planes + s], 0.0)

    before, here = moved(0), moved(1)
    for s in range(1, window - 1):
        after = moved(s + 1)
        value = degree[s] * here - scale[s] * (before + after + two_sided(here))
        once[s] = value
        if REACH <= s < window - REACH:
            kept[pl.ds((s - REACH) * lines * vectors + k, lines, stride=vectors), :] = value[0:lines]
        before, here = here, after
    for s in range(REACH, window - REACH):
        value = once[s]
        result = degree[s] * value - scale[s] * (once[s - 1] + once[s + 1] + two_sided(value))
        image[0, s - REACH] = result[0:lines]

    @pl.when(k == vectors - 1)
    def _():
        rows = 8 * vectors
        steps = band * lines // 8

        def add(step, total):
            block = kept[pl.ds(pl.multiple_of(step * rows, rows), rows), :]
            high = block.astype(jnp.bfloat16)
            low = (block - high.astype(jnp.float32)).astype(jnp.bfloat16)
            dot = functools.partial(
                lax.dot_general, dimension_numbers=(((1,), (1,)), ((), ())), preferred_element_type=jnp.float32
            )
            return total[0] + dot(high, high), total[1] + dot(high, low)

        zero = jnp.zeros((rows, rows), jnp.float32)
        square, cross = lax.fori_loop(0, steps, add, (zero, zero), unroll=4)
        total = square + (cross + cross.T)
        row = lax.broadcasted_iota(jnp.int32, total.shape, 0) // vectors
        column = lax.broadcasted_iota(jnp.int32, total.shape, 1) // vectors
        total = jnp.where(row == column, total, 0.0)
        folded = total[0:vectors]
        for part in range(1, 8):
            folded = folded + total[part * vectors : (part + 1) * vectors]
        shift = rows // 2
        while shift >= vectors:
            folded = folded + pltpu.roll(folded, shift, 1)
            shift //= 2
        gram[...] = folded / slots


def gram_sum_kernel(sides, lane_count, local, out, lane_got, total, chain_got, *sems):
    chain_count = len(sides)
    my_chain, my_lane = lax.axis_index("chain"), lax.axis_index("lane")
    barrier = pltpu.get_barrier_semaphore()
    for d in range(1, lane_count):
        pl.semaphore_signal(barrier, inc=1, device_id=(my_chain, (my_lane + d) % lane_count),
                            device_id_type=pl.DeviceIdType.MESH)
    for d in range(1, chain_count):
        pl.semaphore_signal(barrier, inc=1, device_id=((my_chain + d) % chain_count, my_lane),
                            device_id_type=pl.DeviceIdType.MESH)
    pl.semaphore_wait(barrier, lane_count + chain_count - 2)

    def gather(src, got, me, count, device, send, recv):
        def copy(d, slot):
            return pltpu.make_async_remote_copy(
                src_ref=src, dst_ref=got.at[slot], send_sem=send.at[d], recv_sem=recv.at[d],
                device_id=device((me + d) % count), device_id_type=pl.DeviceIdType.MESH,
            )

        for d in range(1, count):
            copy(d, me).start()
        got[me] = src[...]
        for d in range(1, count):
            copy(d, (me + count - d) % count).wait_recv()
        for d in range(1, count):
            copy(d, me).wait_send()

    gather(local, lane_got, my_lane, lane_count, lambda i: (my_chain, i), sems[0], sems[1])
    value = lane_got[0]
    for i in range(1, lane_count):
        value = value + lane_got[i]
    total[...] = value
    gather(total, chain_got, my_chain, chain_count, lambda i: (i, my_lane), sems[2], sems[3])
    for side in range(2):
        members = [c for c in range(chain_count) if sides[c] == side]
        value = chain_got[members[0]]
        for c in members[1:]:
            value = value + chain_got[c]
        out[side] = value


def per_device(fiedler, side_labels):
    chain_count, lane_count = lax.axis_size("chain"), lax.axis_size("lane")
    vectors, plane_count, lines, width = fiedler.shape
    band, own_slot, bounds, sides, groups = band_plan(chain_count, plane_count)
    me = lax.axis_index("chain")
    slots = band * (chain_count // 2) * lines * lane_count * width
    rows = np.stack(
        [own_slot, bounds[0], bounds[1], sides]
        + [group["arrives"] for group in groups]
        + [group["start"] for group in groups]
    )
    table = lax.optimization_barrier(jnp.asarray(rows.T)[me])
    marks = side_labels.astype(jnp.float32)[None]

    def both(part):
        return jnp.concatenate([part(fiedler), part(marks)], axis=0)

    up = [(i, (i + 1) % lane_count) for i in range(lane_count)]
    down = [(j, i) for i, j in up]
    after = lax.ppermute(both(lambda a: a[:, :, :REACH]), "lane", down)
    before = lax.ppermute(both(lambda a: a[:, :, lines - REACH :]), "lane", up)
    edge = jnp.concatenate([after, before], axis=2)

    counts = tuple(group["count"] for group in groups)
    got, edges_got = [], []
    for which, group in enumerate(groups):
        start = table[4 + len(groups) + which]
        pairs = list(zip(group["sources"], group["targets"]))
        count = group["count"]
        cut = functools.partial(lax.dynamic_slice_in_dim, start_index=start, slice_size=count, axis=1)
        got.append(lax.ppermute(both(cut), "chain", pairs))
        edges_got.append(lax.ppermute(cut(edge), "chain", pairs))

    def spec(shape, at):
        return pl.BlockSpec((1,) + shape[1:], lambda k, t: (k if at is None else at, 0, 0, 0))

    operands = [fiedler, side_labels, edge, edge]
    in_specs = [
        spec(fiedler.shape, None),
        pl.BlockSpec(side_labels.shape, lambda k, t: (0, 0, 0)),
        spec(edge.shape, None),
        spec(edge.shape, vectors),
    ]
    for body, border in zip(got, edges_got):
        operands += [body, body, border, border]
        in_specs += [spec(body.shape, None), spec(body.shape, vectors)]
        in_specs += [spec(border.shape, None), spec(border.shape, vectors)]
    window = band + 2 * REACH
    tall = lines + 8
    held = (plane_count * 2 + window, tall, width)
    image, wide = pl.pallas_call(
        functools.partial(laplace_kernel, counts, plane_count, lines, band, vectors, float(slots)),
        grid_spec=pltpu.PrefetchScalarGridSpec(
            num_scalar_prefetch=1,
            grid=(vectors,),
            in_specs=in_specs,
            out_specs=[
                pl.BlockSpec((1, band, lines, width), lambda k, t: (k, 0, 0, 0)),
                pl.BlockSpec((vectors, 8 * vectors), lambda k, t: (0, 0)),
            ],
            scratch_shapes=[
                pltpu.VMEM(held, jnp.float32),
                pltpu.VMEM(held, jnp.float32),
                pltpu.VMEM((window, tall, width), jnp.float32),
                pltpu.VMEM((window, tall, width), jnp.float32),
                pltpu.VMEM((window, tall, width), jnp.float32),
                pltpu.VMEM((band * lines * vectors, width), jnp.float32),
            ],
        ),
        out_shape=[
            jax.ShapeDtypeStruct((vectors, band, lines, width), jnp.float32),
            jax.ShapeDtypeStruct((vectors, 8 * vectors), jnp.float32),
        ],
        compiler_params=pltpu.CompilerParams(
            dimension_semantics=("arbitrary",), vmem_limit_bytes=48 * 1024 * 1024
        ),
        name="laplace",
    )(table, *operands)
    shape = wide.shape
    sums = pl.pallas_call(
        functools.partial(gram_sum_kernel, tuple(int(side) for side in sides), lane_count),
        out_shape=jax.ShapeDtypeStruct((2,) + shape, jnp.float32),
        in_specs=[pl.BlockSpec(memory_space=pltpu.VMEM)],
        out_specs=pl.BlockSpec(memory_space=pltpu.VMEM),
        scratch_shapes=[
            pltpu.VMEM((lane_count,) + shape, jnp.float32),
            pltpu.VMEM(shape, jnp.float32),
            pltpu.VMEM((chain_count,) + shape, jnp.float32),
            pltpu.SemaphoreType.DMA((lane_count,)),
            pltpu.SemaphoreType.DMA((lane_count,)),
            pltpu.SemaphoreType.DMA((chain_count,)),
            pltpu.SemaphoreType.DMA((chain_count,)),
        ],
        compiler_params=pltpu.CompilerParams(collective_id=0, has_side_effects=True),
        name="gram_sum",
    )(wide)
    return image, sums[:, :, :vectors]


def solution(mesh):
    return jax.shard_map(
        per_device,
        mesh=mesh,
        in_specs=(P(None, "chain", "lane", None), P("chain", "lane", None)),
        out_specs=(P(None, "chain", "lane", None), P()),
        check_vma=False,
    )
```

profile of v0, /device:TPU:1, one launch (start us, length us, event | category | flops | bytes accessed | tf_op | source)
XLA Modules:
  0.0 77.4 jit_solution(3173633500489344008)
XLA Ops:
  0.6 0.7 fusion.3.table
  1.3 0.6 fusion.7
  3.3 1.0 %fusion.5 = (f32[12,32,128]{2,1,0:T(8,128)S(1)}, f32[1,12,32,128]{3,2,1,0:T(8,128)S(1)}) fusion(s32[12,32,128]{2,1,0:T(8,128)} %refs_1_.1), kind=kLoop, calls=%fused_computation.25 | loop fusion | flops 49152 | bytes 589824 | tf_op jit(solution)/shard_map/convert_element_type | solution.py:200
  4.2 0.0 copy-start.2
  4.9 1.6 %constant_dynamic-slice_fusion.2 = f32[16,6,32,128]{3,2,1,0:T(8,128)S(1)} fusion(f32[16,12,32,128]{3,2,1,0:T(8,128)} %refs_0_.1, s32[]{:T(128)S(6)} %select_n.9), kind=kLoop, calls=%fused_computation.20 | loop fusion | bytes 3145732 | tf_op jit(solution)/shard_map/dynamic_slice | solution.py:203
  6.5 1.4 %pad_maximum_fusion = f32[17,6,32,128]{3,2,1,0:T(8,128)} fusion(f32[1,6,32,128]{3,2,1,0:T(8,128)S(1)} %dynamic-slice_bitcast_fusion, f32[16,6,32,128]{3,2,1,0:T(8,128)S(1)} %constant_dynamic-slice_fusion.2), kind=kLoop, calls=%fused_computation | loop fusion | flops 417792 | bytes 3342336 | tf_op jit(solution)/shard_map/concatenate | solution.py:203
  7.9 4.5 %collective-permute-start.2 = (f32[17,6,32,128]{3,2,1,0:T(8,128)}, f32[17,6,32,128]{3,2,1,0:T(8,128)S(1)}, u32[]{:S(2)}, u32[]{:S(2)}) collective-permute-start(f32[17,6,32,128]{3,2,1,0:T(8,128)} %pad_maximum_fusion), channel_id=1, source_target_pairs={{24,20},{20,24},{8,4},{4,8},{25,21},{21,25},{9,5},{5,9},{26,22},{2... | collective-permute-start | bytes 5013512 | tf_op jit(solution)/shard_map/ppermute | solution.py:218
  14.2 0.0 copy-done.2
  14.2 1.4 %constant_dynamic-slice_fusion.1 = f32[16,5,32,128]{3,2,1,0:T(8,128)S(1)} fusion(f32[16,12,32,128]{3,2,1,0:T(8,128)} %refs_0_.1, s32[]{:T(128)S(6)} %select_n.20), kind=kLoop, calls=%fused_computation.19 | loop fusion | bytes 2621444 | tf_op jit(solution)/shard_map/dynamic_slice | solution.py:203
  15.7 1.2 %pad_maximum_fusion.1 = f32[17,5,32,128]{3,2,1,0:T(8,128)} fusion(f32[1,5,32,128]{3,2,1,0:T(8,128)S(1)} %dynamic-slice_bitcast_fusion.1, f32[16,5,32,128]{3,2,1,0:T(8,128)S(1)} %constant_dynamic-slice_fusion.1), kind=kLoop, calls=%fused_computation.1 | loop fusion | flops 348160 | bytes 2785280 | tf_op jit(solution)/shard_map/concatenate | solution.py:203
  16.9 1.4 %collective-permute-start.4 = (f32[17,5,32,128]{3,2,1,0:T(8,128)}, f32[17,5,32,128]{3,2,1,0:T(8,128)S(1)}, u32[]{:S(2)}, u32[]{:S(2)}) collective-permute-start(f32[17,5,32,128]{3,2,1,0:T(8,128)} %pad_maximum_fusion.1), channel_id=1, source_target_pairs={{24,28},{20,16},{8,12},{4,0},{25,29},{21,17},{9,13},{5,1},{26,30},... | collective-permute-start | bytes 4177928 | tf_op jit(solution)/shard_map/ppermute | solution.py:218
  18.3 1.5 %fusion.4 = (f32[16,12,2,128]{3,2,1,0:T(2,128)S(1)}, f32[16,12,2,128]{3,2,1,0:T(2,128)S(1)}) fusion(f32[16,12,32,128]{3,2,1,0:T(8,128)} %refs_0_.1), kind=kLoop, calls=%fused_computation.24 | loop fusion | bytes 786432 | tf_op jit(solution)/shard_map/slice | solution.py:207
  19.8 0.8 %pad_maximum_fusion.5 = f32[17,12,2,128]{3,2,1,0:T(2,128)} fusion(f32[1,12,2,128]{3,2,1,0:T(2,128)S(1)} %get-tuple-element.11, f32[16,12,2,128]{3,2,1,0:T(2,128)S(1)} %get-tuple-element.7), kind=kLoop, calls=%fused_computation.12 | loop fusion | flops 52224 | bytes 417792 | tf_op jit(solution)/shard_map/concatenate | solution.py:203
  20.6 1.3 %collective-permute-start.1 = (f32[17,12,2,128]{3,2,1,0:T(2,128)}, f32[17,12,2,128]{3,2,1,0:T(2,128)S(1)}, u32[]{:S(2)}, u32[]{:S(2)}) collective-permute-start(f32[17,12,2,128]{3,2,1,0:T(2,128)} %pad_maximum_fusion.5), channel_id=1, source_target_pairs={{0,1},{1,2},{2,3},{3,0},{4,5},{5,6},{6,7},{7,4},{8,9},{9,10},{10,1... | collective-permute-start | bytes 626696 | tf_op jit(solution)/shard_map/ppermute | solution.py:208
  21.9 0.8 %pad_maximum_fusion.4 = f32[17,12,2,128]{3,2,1,0:T(2,128)} fusion(f32[1,12,2,128]{3,2,1,0:T(2,128)S(1)} %get-tuple-element.10, f32[16,12,2,128]{3,2,1,0:T(2,128)S(1)} %get-tuple-element.6), kind=kLoop, calls=%fused_computation.11 | loop fusion | flops 52224 | bytes 417792 | tf_op jit(solution)/shard_map/concatenate | solution.py:203
  22.7 2.0 %collective-permute-start = (f32[17,12,2,128]{3,2,1,0:T(2,128)}, f32[17,12,2,128]{3,2,1,0:T(2,128)S(1)}, u32[]{:S(2)}, u32[]{:S(2)}) collective-permute-start(f32[17,12,2,128]{3,2,1,0:T(2,128)} %pad_maximum_fusion.4), channel_id=1, source_target_pairs={{1,0},{2,1},{3,2},{0,3},{5,4},{6,5},{7,6},{4,7},{9,8},{10,9},{11,1... | collective-permute-start | bytes 626696 | tf_op jit(solution)/shard_map/ppermute | solution.py:207
  26.7 1.1 %constant_dynamic-slice_fusion = f32[16,2,32,128]{3,2,1,0:T(8,128)S(1)} fusion(f32[16,12,32,128]{3,2,1,0:T(8,128)} %refs_0_.1, s32[]{:T(128)S(6)} %select_n.21), kind=kLoop, calls=%fused_computation.18 | loop fusion | bytes 1048580 | tf_op jit(solution)/shard_map/dynamic_slice | solution.py:203
  27.8 0.8 dynamic-slice_bitcast_fusion.2
  28.5 0.0 copy-start
  28.6 0.8 %collective-permute-start.6 = (f32[17,2,32,128]{3,2,1,0:T(8,128)S(1)}, f32[17,2,32,128]{3,2,1,0:T(8,128)S(1)}, u32[]{:S(2)}, u32[]{:S(2)}) collective-permute-start(f32[17,2,32,128]{3,2,1,0:T(8,128)S(1)} %pad_maximum_fusion.3), channel_id=1, source_target_pairs={{28,0},{16,12},{12,16},{0,28},{29,1},{17,13},{13,17},{1,29},{30,2}... | collective-permute-start | bytes 1671176 | tf_op jit(solution)/shard_map/ppermute | solution.py:218
  29.4 0.0 collective-permute-done.1
  29.4 2.8 %collective-permute-done = f32[17,12,2,128]{3,2,1,0:T(2,128)S(1)} collective-permute-done((f32[17,12,2,128]{3,2,1,0:T(2,128)}, f32[17,12,2,128]{3,2,1,0:T(2,128)S(1)}, u32[]{:S(2)}, u32[]{:S(2)}) %collective-permute-start) | collective-permute-done | bytes 208928 | tf_op jit(solution)/shard_map/ppermute | solution.py:207
  32.2 0.7 collective-permute-start.7
  32.9 0.1 fusion
  33.0 2.5 %collective-permute-start.3 = (f32[17,6,4,128]{3,2,1,0:T(4,128)S(1)}, f32[17,6,4,128]{3,2,1,0:T(4,128)S(1)}, u32[]{:S(2)}, u32[]{:S(2)}) collective-permute-start(f32[17,6,4,128]{3,2,1,0:T(4,128)S(1)} %fusion), channel_id=1, source_target_pairs={{24,20},{20,24},{8,4},{4,8},{25,21},{21,25},{9,5},{5,9},{26,22},{2... | collective-permute-start | bytes 626696 | tf_op jit(solution)/shard_map/ppermute | solution.py:219
  35.6 0.1 fusion.1
  35.7 0.0 collective-permute-done.7.refs_14_.refs_15_
  35.7 6.6 %collective-permute-start.5 = (f32[17,5,4,128]{3,2,1,0:T(4,128)S(1)}, f32[17,5,4,128]{3,2,1,0:T(4,128)S(1)}, u32[]{:S(2)}, u32[]{:S(2)}) collective-permute-start(f32[17,5,4,128]{3,2,1,0:T(4,128)S(1)} %fusion.1), channel_id=1, source_target_pairs={{24,28},{20,16},{8,12},{4,0},{25,29},{21,17},{9,13},{5,1},{26,30},... | collective-permute-start | bytes 522248 | tf_op jit(solution)/shard_map/ppermute | solution.py:219
  42.3 0.2 pad_maximum_fusion.2.refs_2_.refs_3_
  42.5 0.8 %collective-permute-done.5.refs_10_.refs_11_ = f32[17,5,4,128]{3,2,1,0:T(4,128)S(1)} collective-permute-done((f32[17,5,4,128]{3,2,1,0:T(4,128)S(1)}, f32[17,5,4,128]{3,2,1,0:T(4,128)S(1)}, u32[]{:S(2)}, u32[]{:S(2)}) %collective-permute-start.5) | collective-permute-done | bytes 174112 | tf_op jit(solution)/shard_map/ppermute | solution.py:219
  43.3 0.0 collective-permute-done.3.refs_6_.refs_7_
  43.3 0.0 collective-permute-done.6.refs_12_.refs_13_
  43.3 0.0 collective-permute-done.4.refs_8_.refs_9_
  43.3 0.0 collective-permute-done.2.refs_4_.refs_5_
  43.3 0.0 copy-done
  43.3 19.1 %laplace.1 = (f32[16,15,32,128]{3,2,1,0:T(8,128)}, f32[16,128]{1,0:T(8,128)S(1)}) custom-call(s32[10]{0:T(128)S(1)} %fusion.3.table, f32[16,12,32,128]{3,2,1,0:T(8,128)} %refs_0_.1, s32[12,32,128]{2,1,0:T(8,128)S(1)} %copy-done, f32[17,12,4,128]{3,2,1,0:T(4,128)S(1)} %pad_maximum_fusion.2.refs_2_.refs_3_, ...), custom_call_target="tpu_custom_call" | custom-call | tf_op jit(solution)/shard_map/laplace/pallas_call | solution.py:238
  62.4 0.0 copy-start.1
  62.4 0.6 copy-done.1
  63.0 13.1 %gram_sum.1 = f32[2,16,128]{2,1,0:T(8,128)} custom-call(f32[16,128]{1,0:T(8,128)} %copy-done.1), custom_call_target="tpu_custom_call" | custom-call | tf_op jit(solution)/shard_map/gram_sum/pallas_call | solution.py:267
  76.1 1.3 %copy.6 = f32[2,16,16]{2,1,0:T(8,128)} copy(f32[2,16,16]{2,1,0:T(8,128)} %bitcast.14) | data formatting | bytes 4096
  (5 shorter events, 0.1 us)
Async XLA Ops:
  4.2 10.0 %copy-start.2 = (f32[12,32,128]{2,1,0:T(8,128)}, f32[12,32,128]{2,1,0:T(8,128)S(1)}, u32[]{:S(2)}) copy-start(f32[12,32,128]{2,1,0:T(8,128)S(1)} %get-tuple-element.8) | copy-start | bytes 589828
  7.9 35.4 %collective-permute-start.2 = (f32[17,6,32,128]{3,2,1,0:T(8,128)}, f32[17,6,32,128]{3,2,1,0:T(8,128)S(1)}, u32[]{:S(2)}, u32[]{:S(2)}) collective-permute-start(f32[17,6,32,128]{3,2,1,0:T(8,128)} %pad_maximum_fusion), channel_id=1, source_target_pairs={{24,20},{20,24},{8,4},{4,8},{25,21},{21,25},{9,5},{5,9},{26,22},{2... | collective-permute-start | bytes 5013512 | tf_op jit(solution)/shard_map/ppermute | solution.py:218
  16.9 26.4 %collective-permute-start.4 = (f32[17,5,32,128]{3,2,1,0:T(8,128)}, f32[17,5,32,128]{3,2,1,0:T(8,128)S(1)}, u32[]{:S(2)}, u32[]{:S(2)}) collective-permute-start(f32[17,5,32,128]{3,2,1,0:T(8,128)} %pad_maximum_fusion.1), channel_id=1, source_target_pairs={{24,28},{20,16},{8,12},{4,0},{25,29},{21,17},{9,13},{5,1},{26,30},... | collective-permute-start | bytes 4177928 | tf_op jit(solution)/shard_map/ppermute | solution.py:218
  20.6 8.8 %collective-permute-start.1 = (f32[17,12,2,128]{3,2,1,0:T(2,128)}, f32[17,12,2,128]{3,2,1,0:T(2,128)S(1)}, u32[]{:S(2)}, u32[]{:S(2)}) collective-permute-start(f32[17,12,2,128]{3,2,1,0:T(2,128)} %pad_maximum_fusion.5), channel_id=1, source_target_pairs={{0,1},{1,2},{2,3},{3,0},{4,5},{5,6},{6,7},{7,4},{8,9},{9,10},{10,1... | collective-permute-start | bytes 626696 | tf_op jit(solution)/shard_map/ppermute | solution.py:208
  22.7 9.5 %collective-permute-start = (f32[17,12,2,128]{3,2,1,0:T(2,128)}, f32[17,12,2,128]{3,2,1,0:T(2,128)S(1)}, u32[]{:S(2)}, u32[]{:S(2)}) collective-permute-start(f32[17,12,2,128]{3,2,1,0:T(2,128)} %pad_maximum_fusion.4), channel_id=1, source_target_pairs={{1,0},{2,1},{3,2},{0,3},{5,4},{6,5},{7,6},{4,7},{9,8},{10,9},{11,1... | collective-permute-start | bytes 626696 | tf_op jit(solution)/shard_map/ppermute | solution.py:207
  28.5 14.8 %copy-start = (s32[12,32,128]{2,1,0:T(8,128)S(1)}, s32[12,32,128]{2,1,0:T(8,128)}, u32[]{:S(2)}) copy-start(s32[12,32,128]{2,1,0:T(8,128)} %refs_1_.1) | copy-start | bytes 589828
  28.6 14.7 %collective-permute-start.6 = (f32[17,2,32,128]{3,2,1,0:T(8,128)S(1)}, f32[17,2,32,128]{3,2,1,0:T(8,128)S(1)}, u32[]{:S(2)}, u32[]{:S(2)}) collective-permute-start(f32[17,2,32,128]{3,2,1,0:T(8,128)S(1)} %pad_maximum_fusion.3), channel_id=1, source_target_pairs={{28,0},{16,12},{12,16},{0,28},{29,1},{17,13},{13,17},{1,29},{30,2}... | collective-permute-start | bytes 1671176 | tf_op jit(solution)/shard_map/ppermute | solution.py:218
  32.2 3.4 %collective-permute-start.7 = (f32[17,2,4,128]{3,2,1,0:T(4,128)S(1)}, f32[17,2,4,128]{3,2,1,0:T(4,128)S(1)}, u32[]{:S(2)}, u32[]{:S(2)}) collective-permute-start(f32[17,2,4,128]{3,2,1,0:T(4,128)S(1)} %fusion.2), channel_id=1, source_target_pairs={{28,0},{16,12},{12,16},{0,28},{29,1},{17,13},{13,17},{1,29},{30,2}... | collective-permute-start | bytes 208904 | tf_op jit(solution)/shard_map/ppermute | solution.py:219
  33.0 10.3 %collective-permute-start.3 = (f32[17,6,4,128]{3,2,1,0:T(4,128)S(1)}, f32[17,6,4,128]{3,2,1,0:T(4,128)S(1)}, u32[]{:S(2)}, u32[]{:S(2)}) collective-permute-start(f32[17,6,4,128]{3,2,1,0:T(4,128)S(1)} %fusion), channel_id=1, source_target_pairs={{24,20},{20,24},{8,4},{4,8},{25,21},{21,25},{9,5},{5,9},{26,22},{2... | collective-permute-start | bytes 626696 | tf_op jit(solution)/shard_map/ppermute | solution.py:219
  35.7 7.6 %collective-permute-start.5 = (f32[17,5,4,128]{3,2,1,0:T(4,128)S(1)}, f32[17,5,4,128]{3,2,1,0:T(4,128)S(1)}, u32[]{:S(2)}, u32[]{:S(2)}) collective-permute-start(f32[17,5,4,128]{3,2,1,0:T(4,128)S(1)} %fusion.1), channel_id=1, source_target_pairs={{24,28},{20,16},{8,12},{4,0},{25,29},{21,17},{9,13},{5,1},{26,30},... | collective-permute-start | bytes 522248 | tf_op jit(solution)/shard_map/ppermute | solution.py:219
  62.4 0.6 copy-start.1
where the time goes:
time: 78.8 us; the launch traced here: 77.4 us
  Pallas kernels  32.2 us (41%)
  starting transfers between devices  19.8 us (25%)
  local copies, waits for them, and re-layouts  9.7 us (12%)
  between operations  6.59 us (8%)
  other arithmetic  5.58 us (7%)
  waiting for transfers between devices  3.59 us (5%)
    pallas_call x1, Pallas kernels, per_device(): pl.pallas_call(functools.partial(laplace_kernel, counts, plane_count, lin...  19.1 us
    pallas_call x1, Pallas kernels, per_device(): pl.pallas_call(functools.partial(gram_sum_kernel, tuple((int(side) for si...  13.1 us
    ppermute x3, starting transfers between devices, per_device(): edges_got.append(lax.ppermute(cut(edge), 'chain', pairs))  9.81 us
    ppermute x3, starting transfers between devices, per_device(): got.append(lax.ppermute(both(cut), 'chain', pairs))  6.68 us
    dynamic_slice x6, local copies, waits for them, and re-layouts, both(): return jnp.concatenate([part(fiedler), part(marks)], axis=0)  4.88 us
    concatenate x5, other arithmetic, both(): return jnp.concatenate([part(fiedler), part(marks)], axis=0)  4.19 us
    ppermute x1, waiting for transfers between devices, per_device(): after = lax.ppermute(both(lambda a: a[:, :, :REACH]), 'lane', down)  2.76 us
    ppermute x1, starting transfers between devices, per_device(): after = lax.ppermute(both(lambda a: a[:, :, :REACH]), 'lane', down)  2.03 us
  transfers between devices with their start and end apart: 8, of which 2 were waited for; matrix products, arithmetic and copies ran while one was open for 10% of the time, Pallas kernels for 0%

commit v1 on v0

v1 whole, which is shorter than its diff:
```python
import functools

import jax
import jax.numpy as jnp
from jax import lax
from jax.experimental import pallas as pl
from jax.experimental.pallas import tpu as pltpu
from jax.sharding import PartitionSpec as P

REACH = 2
MESH = pl.DeviceIdType.MESH


def two_sided(field):
    return (
        pltpu.roll(field, 1, 0) + pltpu.roll(field, field.shape[0] - 1, 0)
        + pltpu.roll(field, 1, 1) + pltpu.roll(field, field.shape[1] - 1, 1)
    )


class Plan:
    def __init__(self, chain, lanes, vectors, planes, lines, width):
        self.chain, self.lanes, self.vectors, self.planes, self.lines, self.width = (
            chain, lanes, vectors, planes, lines, width)
        self.half = chain // 2
        self.band = planes + planes // 4
        self.grow = self.band - planes
        self.margin = self.grow * self.half // 2
        self.window = self.band + 2 * REACH
        spots = [self.spot(w, max_of=max) for w in range(self.half)]
        self.most = max(max(below, above) for _, below, above in spots)
        assert self.most <= planes and 8 * vectors == width
        assert spots[0][1] == spots[-1][2] > 0 and spots[0][2] == spots[-1][1] == 0
        self.pad = 1 + max(max(0, -slot) for slot, _, _ in spots)
        tail = 1 + max(max(0, slot + planes - self.window) for slot, _, _ in spots)
        self.frames = self.pad + self.window + tail

    def spot(self, w, max_of=jnp.maximum):
        first, last = (w == 0), (w == self.half - 1)
        if not isinstance(w, int):
            first, last = first.astype(jnp.int32), last.astype(jnp.int32)
        slot = self.margin + REACH - self.grow * w
        below = max_of(0, slot - REACH * first)
        above = max_of(0, self.window - REACH * last - slot - self.planes)
        return slot, below, above

    def place(self, c):
        relative = lax.rem(c + (self.chain - self.chain // 4), self.chain)
        side = lax.div(relative, self.half)
        within = relative - side * self.half
        return side, within


def kernel(plan, scale_of, fiedler, labels, image, gram, field, moved, once, mark, label, count, counted, spare, acc,
           packed, got, local_sem, lab_s, lab_r, own_s, own_r, plane_s, plane_r, edge_s, edge_r, cnt_s, cnt_r,
           gram_s, gram_r):
    chain, lanes, vectors, planes, lines, width = (
        plan.chain, plan.lanes, plan.vectors, plan.planes, plan.lines, plan.width)
    window, pad, most = plan.window, plan.pad, plan.most
    c, l = lax.axis_index("chain"), lax.axis_index("lane")
    up_c, down_c = lax.rem(c + 1, chain), lax.rem(c + chain - 1, chain)
    up_l, down_l = lax.rem(l + 1, lanes), lax.rem(l + lanes - 1, lanes)
    side, within = plan.place(c)
    slot, below, above = plan.spot(within)
    up_side, up_within = plan.place(up_c)
    down_side, down_within = plan.place(down_c)
    up_slot, up_count, _ = plan.spot(up_within)
    down_slot, _, down_count = plan.spot(down_within)
    tall = lines + 8
    lo, hi = slice(0, REACH), slice(lines - REACH, lines)
    nxt, prv = slice(lines, lines + REACH), slice(tall - REACH, tall)

    def remote(src, dst, send, recv, device):
        return pltpu.make_async_remote_copy(
            src_ref=src, dst_ref=dst, send_sem=send, recv_sem=recv, device_id=device, device_id_type=MESH)

    base = pad + slot
    load_field = pltpu.make_async_copy(fiedler, field.at[:, pl.ds(base, planes), 0:lines], local_sem.at[0])
    load_label = pltpu.make_async_copy(labels, label.at[:, 0:lines], local_sem.at[1])
    load_label.start()
    load_field.start()

    barrier = pltpu.get_barrier_semaphore()
    for dc in range(chain):
        for dl in range(lanes):
            if dc or dl:
                pl.semaphore_signal(barrier, inc=1, device_id=(lax.rem(c + dc, chain), lax.rem(l + dl, lanes)),
                                    device_id_type=MESH)
    pl.semaphore_wait(barrier, chain * lanes - 1)

    lab_copies = [
        remote(labels.at[:, lo], label.at[:, nxt], lab_s.at[0], lab_r.at[0], (c, down_l)),
        remote(labels.at[:, hi], label.at[:, prv], lab_s.at[1], lab_r.at[1], (c, up_l)),
    ]
    own = pl.ds(base, planes)
    own_copies = [
        remote(fiedler.at[:, :, lo], field.at[:, own, nxt], own_s.at[0], own_r.at[0], (c, down_l)),
        remote(fiedler.at[:, :, hi], field.at[:, own, prv], own_s.at[1], own_r.at[1], (c, up_l)),
    ]

    def plane_copies(way, j):
        if way == 0:
            source, at, to = planes - j, pad + up_slot - j, up_c
        else:
            source, at, to = j - 1, pad + down_slot + planes - 1 + j, down_c
        return [
            remote(fiedler.at[:, source], field.at[:, at, 0:lines], plane_s.at[way, j - 1], plane_r.at[way, j - 1],
                   (to, l)),
            remote(fiedler.at[:, source, lo], field.at[:, at, nxt], edge_s.at[way, j - 1, 0],
                   edge_r.at[way, j - 1, 0], (to, down_l)),
            remote(fiedler.at[:, source, hi], field.at[:, at, prv], edge_s.at[way, j - 1, 1],
                   edge_r.at[way, j - 1, 1], (to, up_l)),
        ]

    for copy in lab_copies:
        copy.start()
    for j in range(1, most + 1):
        for way, total in ((0, up_count), (1, down_count)):
            @pl.when(j <= total)
            def _():
                for copy in plane_copies(way, j):
                    copy.start()
        if j == 1:
            for copy in own_copies:
                copy.start()

    load_label.wait()
    for copy in lab_copies:
        copy.wait_recv()

    def count_copy(way):
        return remote(count.at[way], counted.at[way], cnt_s.at[way], cnt_r.at[way], ((up_c, down_c)[way], l))

    totals = [jnp.zeros((tall, width), jnp.float32) for _ in range(2)]
    for p in range(planes):
        here = label[p]
        totals[0] += jnp.where((here == up_side) & (p >= planes - up_count), 1.0, 0.0)
        totals[1] += jnp.where((here == down_side) & (p < down_count), 1.0, 0.0)
    for way, total in ((0, up_count), (1, down_count)):
        count[way] = totals[way]

        @pl.when(total > 0)
        def _():
            count_copy(way).start()

    acc[...] = jnp.zeros(acc.shape, jnp.float32)
    for p in range(planes):
        mark[base + p] = jnp.where(label[p] == side, 1.0, 0.0)

    is_end = (within == 0) | (within == plan.half - 1)
    lower = within < plan.half // 2
    d = jnp.where(lower, -1, 1)
    near_way, far_way = jnp.where(lower, 0, 1), jnp.where(lower, 1, 0)
    near, far = jnp.where(lower, below, above), jnp.where(lower, above, below)
    near_edge = jnp.where(lower, base, base + planes - 1)
    far_edge = jnp.where(lower, base + planes - 1, base)

    @pl.when(is_end)
    def _():
        at = near_edge + d * (near + 1)
        mark[at] = jnp.zeros((tall, width), jnp.float32)

        def clear(k, _):
            moved[k, at] = jnp.zeros((tall, width), jnp.float32)
            once[k, at] = jnp.zeros((tall, width), jnp.float32)
            return 0

        lax.fori_loop(0, vectors, clear, 0)

    def take(at):
        keep = mark[at] > 0.5

        def one(k, _):
            moved[k, at] = jnp.where(keep, field[k, at], 0.0)
            return 0

        lax.fori_loop(0, vectors, one, 0, unroll=4)

    def weights(before, here, after):
        scale = here * jnp.float32(1.0 / 6.0)
        return scale * (before + after + two_sided(here)), scale

    def apply_once(s):
        degree, scale = weights(mark[s - 1], mark[s], mark[s + 1])

        def one(k, _):
            here = moved[k, s]
            once[k, s] = degree * here - scale * (moved[k, s - 1] + moved[k, s + 1] + two_sided(here))
            return 0

        lax.fori_loop(0, vectors, one, 0, unroll=4)

    def apply_twice(s):
        degree, scale = weights(mark[s - 1], mark[s], mark[s + 1])

        def one(k, _):
            here = once[k, s]
            value = degree * here - scale * (once[k, s - 1] + once[k, s + 1] + two_sided(here))
            image[k, s - pad - REACH] = value[0:lines]
            return 0

        @pl.when((s >= pad + REACH) & (s < pad + window - REACH))
        def _():
            lax.fori_loop(0, vectors, one, 0, unroll=4)

    def add_gram(read, which):
        block = jnp.concatenate(
            [read(g).reshape(8 * vectors, width) for g in range(lines // 8)], axis=1)
        high = block.astype(jnp.bfloat16)
        low = (block - high.astype(jnp.float32)).astype(jnp.bfloat16)
        dot = functools.partial(
            lax.dot_general, dimension_numbers=(((1,), (1,)), ((), ())), preferred_element_type=jnp.float32)
        acc[which, 0] += dot(high, high)
        acc[which, 1] += dot(high, low)

    def gram_of(s):
        add_gram(lambda g: once[:, s, 8 * g : 8 * g + 8, :], 0)

    load_field.wait()
    for copy in own_copies:
        copy.wait_recv()

    def take_own(p, _):
        take(base + p)
        return 0

    lax.fori_loop(0, planes, take_own, 0)

    def inner_once(s, _):
        apply_once(s)

        @pl.when((s >= pad + REACH) & (s < pad + window - REACH))
        def _():
            gram_of(s)
        return 0

    def inner_twice(s, _):
        apply_twice(s)
        return 0

    first, last = jnp.maximum(base, pad), jnp.minimum(base + planes, pad + window)
    lax.fori_loop(first + 1, last - 1, inner_once, 0)
    lax.fori_loop(first + 2, last - 2, inner_twice, 0)

    for way, total in ((0, below), (1, above)):
        @pl.when(total > 0)
        def _():
            count_copy(way).wait_recv()

    def wait_plane(way, j, at):
        remote(fiedler.at[:, 0], field.at[:, at, 0:lines], plane_s.at[way, j - 1], plane_r.at[way, j - 1],
               (c, l)).wait_recv()
        remote(fiedler.at[:, 0, lo], field.at[:, at, nxt], edge_s.at[way, j - 1, 0], edge_r.at[way, j - 1, 0],
               (c, l)).wait_recv()
        remote(fiedler.at[:, 0, hi], field.at[:, at, prv], edge_s.at[way, j - 1, 1], edge_r.at[way, j - 1, 1],
               (c, l)).wait_recv()

    def near_step(j, _):
        at = near_edge + d * j

        @pl.when(j <= near)
        def _():
            wait_plane(near_way, j, at)
            mark[at] = jnp.where(counted[near_way] >= j.astype(jnp.float32) - 0.5, 1.0, 0.0)
            take(at)

        @pl.when(j <= near + 1)
        def _():
            apply_once(at - d)

        @pl.when((at - d >= pad + REACH) & (at - d < pad + window - REACH) & (jnp.logical_not(is_end) | (j == 1)))
        def _():
            gram_of(at - d)

        apply_twice(at - 2 * d)
        return 0

    def far_step(j, _):
        at = far_edge - d * j
        wait_plane(far_way, j, at)
        mark[at] = jnp.where(counted[far_way] >= (far - j + 1).astype(jnp.float32) - 0.5, 1.0, 0.0)
        take(at)
        apply_once(at + d)

        @pl.when((at + d >= pad + REACH) & (at + d < pad + window - REACH))
        def _():
            gram_of(at + d)

        apply_twice(at + 2 * d)
        return 0

    def other_step(j, _):
        at = near_edge - d * (j - 1)
        toward, away = 1.0 - mark[at + d], jnp.where(j < near, 1.0 - mark[at - d], 0.0)
        here = 1.0 - mark[at]
        degree, scale = weights(toward, here, away)

        def one(k, _):
            def part(keep, index):
                return jnp.where(keep > 0.5, field[k, index], 0.0)

            value = part(here, at)
            value = degree * value - scale * (part(toward, at + d) + part(away, at - d) + two_sided(value))
            spare[k] = value[0:lines]
            return 0

        lax.fori_loop(0, vectors, one, 0, unroll=4)
        add_gram(lambda g: spare[:, 8 * g : 8 * g + 8, :], 1)
        return 0

    early = jnp.where(is_end, jnp.minimum(near, 1), near) + 1
    lax.fori_loop(1, early, near_step, 0)

    @pl.when(is_end)
    def _():
        lax.fori_loop(1, near + 1, other_step, 0)

    lax.fori_loop(1, far + 1, far_step, 0)

    me = c * lanes + l
    lane_of = functools.partial(lax.broadcasted_iota, jnp.int32)
    for which in range(2):
        total = acc[which, 0] + (acc[which, 1] + acc[which, 1].T)
        shape = (vectors, 8, width)
        diagonal = lane_of(shape, 1) == lax.rem(lane_of(shape, 2), 8)
        rows = jnp.sum(jnp.where(diagonal, total.reshape(shape), 0.0), axis=1)
        ones = jnp.where(lax.div(lane_of((width, width), 0), 8) == lax.div(lane_of((width, width), 1), 8), 1.0, 0.0)
        rows = jnp.dot(rows, ones, precision=lax.Precision.HIGHEST, preferred_element_type=jnp.float32)
        half = (8, width)
        pick = lane_of(half, 0) == lax.rem(lane_of(half, 1), 8)
        for h in range(vectors // 8):
            row = jnp.sum(jnp.where(pick, rows[8 * h : 8 * h + 8], 0.0), axis=0, keepdims=True)
            for place in range(2):
                @pl.when((side if which == 0 else 1 - side) == place)
                def _():
                    packed[place * (vectors // 8) + h : place * (vectors // 8) + h + 1, :] = row
    count_rows = 2 * (vectors // 8)
    body = packed.at[0:count_rows]
    for dc in range(chain):
        for dl in range(lanes):
            if dc or dl:
                remote(body, got.at[me, 0:count_rows], gram_s.at[0], gram_r.at[0],
                       (lax.rem(c + dc, chain), lax.rem(l + dl, lanes))).start()
    got[me, 0:count_rows] = packed[0:count_rows]

    lax.fori_loop(early, near, near_step, 0)

    everyone = got.at[0 : chain * lanes - 1, 0:count_rows]
    remote(everyone, everyone, gram_s.at[0], gram_r.at[0], (c, l)).wait_recv()

    def sum_one(i, total):
        return total + got[i, 0:count_rows]

    total = lax.fori_loop(1, chain * lanes, sum_one, got[0, 0:count_rows], unroll=True)
    tall_shape = (vectors, width)
    inside = lax.div(lane_of(tall_shape, 1), 8) == lane_of(tall_shape, 0)
    choose = jnp.where(
        lax.rem(lane_of((width, width), 0), 8) == lax.rem(lane_of((width, width), 1), 8), 1.0, 0.0)
    for place in range(2):
        result = jnp.zeros(tall_shape, jnp.float32)
        for h in range(vectors // 8):
            i = place * (vectors // 8) + h
            spread = jnp.where(inside, jnp.broadcast_to(total[i : i + 1], tall_shape), 0.0)
            spread = jnp.dot(spread, choose, precision=lax.Precision.HIGHEST, preferred_element_type=jnp.float32)
            result = jnp.where(lax.div(lane_of(tall_shape, 1), 8) == h, spread, result)
        gram[place] = result[:, 0:vectors] / scale_of

    lax.fori_loop(jnp.maximum(early, near), near + 1 + 2 * is_end.astype(jnp.int32), near_step, 0)

    remote(everyone, everyone, gram_s.at[0], gram_r.at[0], (c, l)).wait_send()
    for copy in lab_copies + own_copies:
        copy.wait_send()
    for way, total in ((0, up_count), (1, down_count)):
        @pl.when(total > 0)
        def _():
            count_copy(way).wait_send()
        for j in range(1, most + 1):
            @pl.when(j <= total)
            def _():
                for copy in plane_copies(way, j):
                    copy.wait_send()


def per_device(fiedler, side_labels):
    chain, lanes = lax.axis_size("chain"), lax.axis_size("lane")
    vectors, planes, lines, width = fiedler.shape
    plan = Plan(chain, lanes, vectors, planes, lines, width)
    slots = plan.band * plan.half * lines * lanes * width
    tall, frames, most = lines + 8, plan.frames, plan.most
    f32, dma = jnp.float32, pltpu.SemaphoreType.DMA
    anywhere, vmem = pl.BlockSpec(memory_space=pl.ANY), pl.BlockSpec(memory_space=pltpu.VMEM)
    return pl.pallas_call(
        functools.partial(kernel, plan, float(slots)),
        in_specs=[anywhere, anywhere],
        out_specs=[vmem, vmem],
        out_shape=[
            jax.ShapeDtypeStruct((vectors, plan.band, lines, width), f32),
            jax.ShapeDtypeStruct((2, vectors, vectors), f32),
        ],
        scratch_shapes=[
            pltpu.VMEM((vectors, frames, tall, width), f32),
            pltpu.VMEM((vectors, frames, tall, width), f32),
            pltpu.VMEM((vectors, frames, tall, width), f32),
            pltpu.VMEM((frames, tall, width), f32),
            pltpu.VMEM((planes, tall, width), jnp.int32),
            pltpu.VMEM((2, tall, width), f32),
            pltpu.VMEM((2, tall, width), f32),
            pltpu.VMEM((vectors, lines, width), f32),
            pltpu.VMEM((2, 2, 8 * vectors, 8 * vectors), f32),
            pltpu.VMEM((8, width), f32),
            pltpu.VMEM((chain * lanes, 8, width), f32),
            dma((2,)), dma((2,)), dma((2,)), dma((2,)), dma((2,)),
            dma((2, most)), dma((2, most)), dma((2, most, 2)), dma((2, most, 2)),
            dma((2,)), dma((2,)), dma((1,)), dma((1,)),
        ],
        compiler_params=pltpu.CompilerParams(
            collective_id=0, has_side_effects=True, vmem_limit_bytes=56 * 1024 * 1024),
        name="laplace",
    )(fiedler, side_labels)


def solution(mesh):
    return jax.shard_map(
        per_device,
        mesh=mesh,
        in_specs=(P(None, "chain", "lane", None), P("chain", "lane", None)),
        out_specs=(P(None, "chain", "lane", None), P()),
        check_vma=False,
    )
```

time: 78.8 us -> 56.8 us (0.72); the launches traced: 77.4 us -> 56.6 us
  starting transfers between devices: 19.8 us -> 0 us
  Pallas kernels: 32.2 us -> 50.9 us
  between operations: 6.59 us -> 0.65 us
  other arithmetic: 5.58 us -> 0 us
  local copies, waits for them, and re-layouts: 9.7 us -> 5.11 us
  waiting for transfers between devices: 3.59 us -> 0 us
    ppermute x8 -> x0, starting transfers between devices: 19.8 us -> none  [the longest x3 9.81 us: per_device(): edges_got.append(lax.ppermute(cut(edge), 'chain', pairs))]
    pallas_call x2 -> x1, Pallas kernels: 32.2 us -> 50.9 us  [per_device(): pl.pallas_call(functools.partial(kernel, plan, float(slots)), in_specs=[a...]
    dynamic_slice x6 -> x0, local copies, waits for them, and re-layouts: 4.88 us -> none  [both(): return jnp.concatenate([part(fiedler), part(marks)], axis=0)]
    concatenate x9 -> x0, other arithmetic: 4.61 us -> none  [the longest x5 4.19 us: both(): return jnp.concatenate([part(fiedler), part(marks)], axis=0)]
    ppermute x8 -> x0, waiting for transfers between devices: 3.59 us -> none  [the longest x1 2.76 us: per_device(): after = lax.ppermute(both(lambda a: a[:, :, :REACH]), 'lane', down)]
    unnamed x7 -> x4, local copies, waits for them, and re-layouts: 1.93 us -> 5.11 us
    slice x3 -> x0, local copies, waits for them, and re-layouts: 2.18 us -> none  [the longest x2 1.54 us: per_device(): after = lax.ppermute(both(lambda a: a[:, :, :REACH]), 'lane', down)]
    convert_element_type x1 -> x0, other arithmetic: 0.96 us -> none  [per_device(): marks = side_labels.astype(jnp.float32)[None]]
  transfers between devices with their start and end apart: 8 -> 0, of which waited for: 2 -> 0; matrix products, arithmetic and copies ran while one was open for 10% -> 0% of each run, Pallas kernels for 0% -> 0%
where the time goes in v1:
time: 56.8 us; the launch traced here: 56.6 us
  Pallas kernels  50.9 us (90%)
  local copies, waits for them, and re-layouts  5.11 us (9%)
  between operations  0.65 us (1%)
    pallas_call x1, Pallas kernels, per_device(): pl.pallas_call(functools.partial(kernel, plan, float(slots)), in_specs=[a...  50.9 us
    unnamed x4, local copies, waits for them, and re-layouts  5.11 us

profile of v1, /device:TPU:1, one launch (start us, length us, event | category | flops | bytes accessed | tf_op | source)
XLA Modules:
  0.0 56.6 jit_solution(8776111949246293513)
XLA Ops:
  0.6 50.9 %laplace.1 = (f32[16,15,32,128]{3,2,1,0:T(8,128)}, f32[2,16,16]{2,1,0:T(8,128)}) custom-call(f32[16,12,32,128]{3,2,1,0:T(8,128)} %fiedler.1, s32[12,32,128]{2,1,0:T(8,128)} %labels.1), custom_call_target="tpu_custom_call" | custom-call | tf_op jit(solution)/shard_map/laplace/pallas_call | solution.py:392
  51.5 0.0 copy-start
  51.5 4.5 %copy.6 = f32[16,15,32,128]{3,2,1,0:T(8,128)} copy(f32[16,15,32,128]{3,2,1,0:T(8,128)} %get-tuple-element.4) | data formatting | bytes 7864320
  56.0 0.0 copy-done
  56.0 0.6 %copy.7 = f32[2,16,16]{2,1,0:T(8,128)} copy(f32[2,16,16]{2,1,0:T(8,128)S(1)} %copy-done) | data formatting | bytes 4096
Async XLA Ops:
  51.5 4.5 %copy-start = (f32[2,16,16]{2,1,0:T(8,128)S(1)}, f32[2,16,16]{2,1,0:T(8,128)}, u32[]{:S(2)}) copy-start(f32[2,16,16]{2,1,0:T(8,128)} %get-tuple-element.5) | copy-start | bytes 6148

commit v2 on v1

--- a/solution.py
+++ b/solution.py
@@ -174,7 +174,7 @@
             moved[k, at] = jnp.where(keep, field[k, at], 0.0)
             return 0
 
-        lax.fori_loop(0, vectors, one, 0, unroll=4)
+        lax.fori_loop(0, vectors, one, 0, unroll=vectors)
 
     def weights(before, here, after):
         scale = here * jnp.float32(1.0 / 6.0)
@@ -188,7 +188,7 @@
             once[k, s] = degree * here - scale * (moved[k, s - 1] + moved[k, s + 1] + two_sided(here))
             return 0
 
-        lax.fori_loop(0, vectors, one, 0, unroll=4)
+        lax.fori_loop(0, vectors, one, 0, unroll=vectors)
 
     def apply_twice(s):
         degree, scale = weights(mark[s - 1], mark[s], mark[s + 1])
@@ -201,7 +201,7 @@
 
         @pl.when((s >= pad + REACH) & (s < pad + window - REACH))
         def _():
-            lax.fori_loop(0, vectors, one, 0, unroll=4)
+            lax.fori_loop(0, vectors, one, 0, unroll=vectors)
 
     def add_gram(read, which):
         block = jnp.concatenate(
@@ -304,7 +304,7 @@
             spare[k] = value[0:lines]
             return 0
 
-        lax.fori_loop(0, vectors, one, 0, unroll=4)
+        lax.fori_loop(0, vectors, one, 0, unroll=vectors)
         add_gram(lambda g: spare[:, 8 * g : 8 * g + 8, :], 1)
         return 0
 
@@ -394,7 +394,7 @@
         in_specs=[anywhere, anywhere],
         out_specs=[vmem, vmem],
         out_shape=[
-            jax.ShapeDtypeStruct((vectors, plan.band, lines, width), f32),
+            pltpu.VMEM((vectors, plan.band, lines, width), f32),
             jax.ShapeDtypeStruct((2, vectors, vectors), f32),
         ],
         scratch_shapes=[

time: 56.8 us -> 48.6 us (0.86)
  Pallas kernels: 50.9 us -> 45.2 us
  local copies, waits for them, and re-layouts: 5.11 us -> 2.53 us
    pallas_call x1, Pallas kernels: 50.9 us -> 45.2 us  [per_device(): pl.pallas_call(functools.partial(kernel, plan, float(slots)), in_specs=[a...]
    unnamed x4, local copies, waits for them, and re-layouts: 5.11 us -> 2.53 us
where the time goes in v2:
time: 48.6 us; the launch traced here: 48.4 us
  Pallas kernels  45.2 us (93%)
  local copies, waits for them, and re-layouts  2.53 us (5%)
  between operations  0.65 us (1%)
    pallas_call x1, Pallas kernels, per_device(): pl.pallas_call(functools.partial(kernel, plan, float(slots)), in_specs=[a...  45.2 us
    unnamed x4, local copies, waits for them, and re-layouts  2.53 us

profile of v2, /device:TPU:1, one launch (start us, length us, event | category | flops | bytes accessed | tf_op | source)
XLA Modules:
  0.0 48.4 jit_solution(12167530031264413438)
XLA Ops:
  0.6 45.2 %laplace.1 = (f32[16,15,32,128]{3,2,1,0:T(8,128)S(1)}, f32[2,16,16]{2,1,0:T(8,128)}) custom-call(f32[16,12,32,128]{3,2,1,0:T(8,128)} %fiedler.1, s32[12,32,128]{2,1,0:T(8,128)} %labels.1), custom_call_target="tpu_custom_call" | custom-call | tf_op jit(solution)/shard_map/laplace/pallas_call | solution.py:392
  45.9 0.0 copy-start
  45.9 1.9 %copy.6 = f32[16,15,32,128]{3,2,1,0:T(8,128)} copy(f32[16,15,32,128]{3,2,1,0:T(8,128)S(1)} %get-tuple-element.2) | data formatting | bytes 7864320
  47.8 0.0 copy-done
  47.8 0.6 %copy.7 = f32[2,16,16]{2,1,0:T(8,128)} copy(f32[2,16,16]{2,1,0:T(8,128)S(1)} %copy-done) | data formatting | bytes 4096
Async XLA Ops:
  45.9 1.9 %copy-start = (f32[2,16,16]{2,1,0:T(8,128)S(1)}, f32[2,16,16]{2,1,0:T(8,128)}, u32[]{:S(2)}) copy-start(f32[2,16,16]{2,1,0:T(8,128)} %get-tuple-element.7) | copy-start | bytes 6148

commit v3 on v2

--- a/solution.py
+++ b/solution.py
@@ -8,6 +8,8 @@
 from jax.sharding import PartitionSpec as P
 
 REACH = 2
+EARLY_PLANES = 3
+CHUNKS = 3
 MESH = pl.DeviceIdType.MESH
 
 
@@ -31,6 +33,9 @@
         self.most = max(max(below, above) for _, below, above in spots)
         assert self.most <= planes and 8 * vectors == width
         assert spots[0][1] == spots[-1][2] > 0 and spots[0][2] == spots[-1][1] == 0
+        self.end_near = spots[0][1]
+        self.chunk = planes // CHUNKS
+        assert self.chunk * CHUNKS == planes and self.chunk > 2
         self.pad = 1 + max(max(0, -slot) for slot, _, _ in spots)
         tail = 1 + max(max(0, slot + planes - self.window) for slot, _, _ in spots)
         self.frames = self.pad + self.window + tail
@@ -52,7 +57,7 @@
 
 
 def kernel(plan, scale_of, fiedler, labels, image, gram, field, moved, once, mark, label, count, counted, spare, acc,
-           packed, got, local_sem, lab_s, lab_r, own_s, own_r, plane_s, plane_r, edge_s, edge_r, cnt_s, cnt_r,
+           packed, got, local_sem, lab_s, lab_r, own_s, own_r, plane_s, plane_r, edge_s, edge_r, pass_s, cnt_s, cnt_r,
            gram_s, gram_r):
     chain, lanes, vectors, planes, lines, width = (
         plan.chain, plan.lanes, plan.vectors, plan.planes, plan.lines, plan.width)
@@ -75,6 +80,14 @@
             src_ref=src, dst_ref=dst, send_sem=send, recv_sem=recv, device_id=device, device_id_type=MESH)
 
     base = pad + slot
+    is_end = (within == 0) | (within == plan.half - 1)
+    lower = within < plan.half // 2
+    d = jnp.where(lower, -1, 1)
+    near_way, far_way = jnp.where(lower, 0, 1), jnp.where(lower, 1, 0)
+    near, far = jnp.where(lower, below, above), jnp.where(lower, above, below)
+    near_edge = jnp.where(lower, base, base + planes - 1)
+    far_edge = jnp.where(lower, base + planes - 1, base)
+
     load_field = pltpu.make_async_copy(fiedler, field.at[:, pl.ds(base, planes), 0:lines], local_sem.at[0])
     load_label = pltpu.make_async_copy(labels, label.at[:, 0:lines], local_sem.at[1])
     load_label.start()
@@ -92,37 +105,68 @@
         remote(labels.at[:, lo], label.at[:, nxt], lab_s.at[0], lab_r.at[0], (c, down_l)),
         remote(labels.at[:, hi], label.at[:, prv], lab_s.at[1], lab_r.at[1], (c, up_l)),
     ]
-    own = pl.ds(base, planes)
-    own_copies = [
-        remote(fiedler.at[:, :, lo], field.at[:, own, nxt], own_s.at[0], own_r.at[0], (c, down_l)),
-        remote(fiedler.at[:, :, hi], field.at[:, own, prv], own_s.at[1], own_r.at[1], (c, up_l)),
-    ]
-
-    def plane_copies(way, j):
+    chunk = plan.chunk
+
+    def own_copies(i):
+        start = jnp.where(lower, i * chunk, planes - (i + 1) * chunk)
+        source, at = pl.ds(start, chunk), pl.ds(base + start, chunk)
+        return [
+            remote(fiedler.at[:, source, lo], field.at[:, at, nxt], own_s.at[i, 0], own_r.at[i, 0], (c, down_l)),
+            remote(fiedler.at[:, source, hi], field.at[:, at, prv], own_s.at[i, 1], own_r.at[i, 1], (c, up_l)),
+        ]
+
+    sends = ((0, up_count, up_side != side), (1, down_count, down_side != side))
+
+    def spot_of(way, j):
         if way == 0:
-            source, at, to = planes - j, pad + up_slot - j, up_c
-        else:
-            source, at, to = j - 1, pad + down_slot + planes - 1 + j, down_c
+            return planes - j, pad + up_slot - j, up_c
+        return j - 1, pad + down_slot + planes - 1 + j, down_c
+
+    def plane_copy(way, j):
+        source, at, to = spot_of(way, j)
+        return remote(
+            fiedler.at[:, source], field.at[:, at, 0:lines], plane_s.at[way, j - 1], plane_r.at[way, j - 1], (to, l))
+
+    def corner_copies(way, j):
+        source, at, to = spot_of(way, j)
         return [
-            remote(fiedler.at[:, source], field.at[:, at, 0:lines], plane_s.at[way, j - 1], plane_r.at[way, j - 1],
-                   (to, l)),
             remote(fiedler.at[:, source, lo], field.at[:, at, nxt], edge_s.at[way, j - 1, 0],
                    edge_r.at[way, j - 1, 0], (to, down_l)),
             remote(fiedler.at[:, source, hi], field.at[:, at, prv], edge_s.at[way, j - 1, 1],
                    edge_r.at[way, j - 1, 1], (to, up_l)),
         ]
 
+    def passed_on(j, total):
+        return (j >= 2) & (j <= total - 2)
+
+    def pass_copies(j):
+        at = near_edge + d * j
+        return [
+            remote(field.at[:, at, lo], field.at[:, at, nxt], pass_s.at[j - 1, 0], edge_r.at[near_way, j - 1, 0],
+                   (c, down_l)),
+            remote(field.at[:, at, hi], field.at[:, at, prv], pass_s.at[j - 1, 1], edge_r.at[near_way, j - 1, 1],
+                   (c, up_l)),
+        ]
+
+    def send_plane(j, late):
+        for way, total, across in sends:
+            @pl.when((j <= total) & (across if late else (jnp.logical_not(across) | (j <= EARLY_PLANES))))
+            def _():
+                plane_copy(way, j).start()
+
+                @pl.when(jnp.logical_not(across & passed_on(j, total)))
+                def _():
+                    for copy in corner_copies(way, j):
+                        copy.start()
+
     for copy in lab_copies:
         copy.start()
-    for j in range(1, most + 1):
-        for way, total in ((0, up_count), (1, down_count)):
-            @pl.when(j <= total)
-            def _():
-                for copy in plane_copies(way, j):
-                    copy.start()
-        if j == 1:
-            for copy in own_copies:
-                copy.start()
+    send_plane(1, False)
+    for i in range(CHUNKS):
+        for copy in own_copies(i):
+            copy.start()
+    for j in range(2, most + 1):
+        send_plane(j, False)
 
     load_label.wait()
     for copy in lab_copies:
@@ -147,14 +191,6 @@
     for p in range(planes):
         mark[base + p] = jnp.where(label[p] == side, 1.0, 0.0)
 
-    is_end = (within == 0) | (within == plan.half - 1)
-    lower = within < plan.half // 2
-    d = jnp.where(lower, -1, 1)
-    near_way, far_way = jnp.where(lower, 0, 1), jnp.where(lower, 1, 0)
-    near, far = jnp.where(lower, below, above), jnp.where(lower, above, below)
-    near_edge = jnp.where(lower, base, base + planes - 1)
-    far_edge = jnp.where(lower, base + planes - 1, base)
-
     @pl.when(is_end)
     def _():
         at = near_edge + d * (near + 1)
@@ -199,7 +235,7 @@
             image[k, s - pad - REACH] = value[0:lines]
             return 0
 
-        @pl.when((s >= pad + REACH) & (s < pad + window - REACH))
+        @pl.when(in_band(s))
         def _():
             lax.fori_loop(0, vectors, one, 0, unroll=vectors)
 
@@ -216,51 +252,25 @@
     def gram_of(s):
         add_gram(lambda g: once[:, s, 8 * g : 8 * g + 8, :], 0)
 
-    load_field.wait()
-    for copy in own_copies:
-        copy.wait_recv()
-
-    def take_own(p, _):
-        take(base + p)
-        return 0
-
-    lax.fori_loop(0, planes, take_own, 0)
-
-    def inner_once(s, _):
-        apply_once(s)
-
-        @pl.when((s >= pad + REACH) & (s < pad + window - REACH))
-        def _():
-            gram_of(s)
-        return 0
-
-    def inner_twice(s, _):
-        apply_twice(s)
-        return 0
-
-    first, last = jnp.maximum(base, pad), jnp.minimum(base + planes, pad + window)
-    lax.fori_loop(first + 1, last - 1, inner_once, 0)
-    lax.fori_loop(first + 2, last - 2, inner_twice, 0)
-
-    for way, total in ((0, below), (1, above)):
-        @pl.when(total > 0)
-        def _():
-            count_copy(way).wait_recv()
+    def in_band(s):
+        return (s >= pad + REACH) & (s < pad + window - REACH)
 
     def wait_plane(way, j, at):
         remote(fiedler.at[:, 0], field.at[:, at, 0:lines], plane_s.at[way, j - 1], plane_r.at[way, j - 1],
                (c, l)).wait_recv()
+
+    def wait_edges(way, j, at):
         remote(fiedler.at[:, 0, lo], field.at[:, at, nxt], edge_s.at[way, j - 1, 0], edge_r.at[way, j - 1, 0],
                (c, l)).wait_recv()
         remote(fiedler.at[:, 0, hi], field.at[:, at, prv], edge_s.at[way, j - 1, 1], edge_r.at[way, j - 1, 1],
                (c, l)).wait_recv()
 
-    def near_step(j, _):
+    def near_use(j, _):
         at = near_edge + d * j
 
         @pl.when(j <= near)
         def _():
-            wait_plane(near_way, j, at)
+            wait_edges(near_way, j, at)
             mark[at] = jnp.where(counted[near_way] >= j.astype(jnp.float32) - 0.5, 1.0, 0.0)
             take(at)
 
@@ -268,21 +278,38 @@
         def _():
             apply_once(at - d)
 
-        @pl.when((at - d >= pad + REACH) & (at - d < pad + window - REACH) & (jnp.logical_not(is_end) | (j == 1)))
+        @pl.when(in_band(at - d) & (jnp.logical_not(is_end) | (j == 1)))
         def _():
             gram_of(at - d)
 
         apply_twice(at - 2 * d)
+        return 0
+
+    def near_step(j, _):
+        goes_on = is_end & passed_on(j, near)
+
+        @pl.when(j <= near)
+        def _():
+            wait_plane(near_way, j, near_edge + d * j)
+
+        @pl.when(goes_on)
+        def _():
+            for copy in pass_copies(j):
+                copy.start()
+
+        begin = jnp.where(is_end & passed_on(j - 1, near), j - 1, j)
+        lax.fori_loop(begin, jnp.where(goes_on, j, j + 1), near_use, 0)
         return 0
 
     def far_step(j, _):
         at = far_edge - d * j
         wait_plane(far_way, j, at)
+        wait_edges(far_way, j, at)
         mark[at] = jnp.where(counted[far_way] >= (far - j + 1).astype(jnp.float32) - 0.5, 1.0, 0.0)
         take(at)
         apply_once(at + d)
 
-        @pl.when((at + d >= pad + REACH) & (at + d < pad + window - REACH))
+        @pl.when(in_band(at + d))
         def _():
             gram_of(at + d)
 
@@ -308,12 +335,51 @@
         add_gram(lambda g: spare[:, 8 * g : 8 * g + 8, :], 1)
         return 0
 
-    early = jnp.where(is_end, jnp.minimum(near, 1), near) + 1
-    lax.fori_loop(1, early, near_step, 0)
-
-    @pl.when(is_end)
+    def take_own(m, _):
+        take(near_edge - d * m)
+        return 0
+
+    def inner_once(m, _):
+        s = near_edge - d * m
+
+        @pl.when((s > pad) & (s < pad + window - 1))
+        def _():
+            apply_once(s)
+
+        @pl.when(in_band(s))
+        def _():
+            gram_of(s)
+        return 0
+
+    def inner_twice(m, _):
+        apply_twice(near_edge - d * m)
+        return 0
+
+    def end_gram():
+        @pl.when(is_end)
+        def _():
+            lax.fori_loop(1, 2, near_step, 0)
+            lax.fori_loop(1, near + 1, other_step, 0)
+
+    load_field.wait()
+    ready = min(CHUNKS - 1, plan.end_near // chunk)
+    for i in range(CHUNKS):
+        for copy in own_copies(i):
+            copy.wait_recv()
+        lax.fori_loop(i * chunk, (i + 1) * chunk, take_own, 0)
+        lax.fori_loop(max(1, i * chunk - 1), (i + 1) * chunk - 1, inner_once, 0)
+        if i == 0:
+            for way, total in ((0, below), (1, above)):
+                @pl.when(total > 0)
+                def _():
+                    count_copy(way).wait_recv()
+        if i == ready:
+            end_gram()
+
+    @pl.when(jnp.logical_not(is_end))
     def _():
-        lax.fori_loop(1, near + 1, other_step, 0)
+        lax.fori_loop(2, planes - 2, inner_twice, 0)
+        lax.fori_loop(1, near + 1, near_step, 0)
 
     lax.fori_loop(1, far + 1, far_step, 0)
 
@@ -343,7 +409,13 @@
                        (lax.rem(c + dc, chain), lax.rem(l + dl, lanes))).start()
     got[me, 0:count_rows] = packed[0:count_rows]
 
-    lax.fori_loop(early, near, near_step, 0)
+    for j in range(EARLY_PLANES + 1, most + 1):
+        send_plane(j, True)
+
+    @pl.when(is_end)
+    def _():
+        lax.fori_loop(2, planes - 2, inner_twice, 0)
+        lax.fori_loop(2, near, near_step, 0)
 
     everyone = got.at[0 : chain * lanes - 1, 0:count_rows]
     remote(everyone, everyone, gram_s.at[0], gram_r.at[0], (c, l)).wait_recv()
@@ -365,20 +437,34 @@
             result = jnp.where(lax.div(lane_of(tall_shape, 1), 8) == h, spread, result)
         gram[place] = result[:, 0:vectors] / scale_of
 
-    lax.fori_loop(jnp.maximum(early, near), near + 1 + 2 * is_end.astype(jnp.int32), near_step, 0)
+    @pl.when(is_end)
+    def _():
+        lax.fori_loop(near, near + 3, near_step, 0)
 
     remote(everyone, everyone, gram_s.at[0], gram_r.at[0], (c, l)).wait_send()
-    for copy in lab_copies + own_copies:
+    for i in range(CHUNKS):
+        for copy in own_copies(i):
+            copy.wait_send()
+    for copy in lab_copies:
         copy.wait_send()
-    for way, total in ((0, up_count), (1, down_count)):
+    for way, total, across in sends:
         @pl.when(total > 0)
         def _():
             count_copy(way).wait_send()
         for j in range(1, most + 1):
             @pl.when(j <= total)
             def _():
-                for copy in plane_copies(way, j):
-                    copy.wait_send()
+                plane_copy(way, j).wait_send()
+
+                @pl.when(jnp.logical_not(across & passed_on(j, total)))
+                def _():
+                    for copy in corner_copies(way, j):
+                        copy.wait_send()
+    for j in range(1, most + 1):
+        @pl.when(is_end & passed_on(j, near))
+        def _():
+            for copy in pass_copies(j):
+                copy.wait_send()
 
 
 def per_device(fiedler, side_labels):
@@ -409,8 +495,8 @@
             pltpu.VMEM((2, 2, 8 * vectors, 8 * vectors), f32),
             pltpu.VMEM((8, width), f32),
             pltpu.VMEM((chain * lanes, 8, width), f32),
-            dma((2,)), dma((2,)), dma((2,)), dma((2,)), dma((2,)),
-            dma((2, most)), dma((2, most)), dma((2, most, 2)), dma((2, most, 2)),
+            dma((2,)), dma((2,)), dma((2,)), dma((CHUNKS, 2)), dma((CHUNKS, 2)),
+            dma((2, most)), dma((2, most)), dma((2, most, 2)), dma((2, most, 2)), dma((most, 2)),
             dma((2,)), dma((2,)), dma((1,)), dma((1,)),
         ],
         compiler_params=pltpu.CompilerParams(

time: 48.6 us -> 51.1 us (1.051)
  Pallas kernels: 45.2 us -> 47.7 us
    pallas_call x1, Pallas kernels: 45.2 us -> 47.7 us  [per_device(): pl.pallas_call(functools.partial(kernel, plan, float(slots)), in_specs=[a...]
where the time goes in v3:
time: 51.1 us; the launch traced here: 50.9 us
  Pallas kernels  47.7 us (93%)
  local copies, waits for them, and re-layouts  2.53 us (5%)
  between operations  0.65 us (1%)
    pallas_call x1, Pallas kernels, per_device(): pl.pallas_call(functools.partial(kernel, plan, float(slots)), in_specs=[a...  47.7 us
    unnamed x4, local copies, waits for them, and re-layouts  2.53 us

profile of v3, /device:TPU:1, one launch (start us, length us, event | category | flops | bytes accessed | tf_op | source)
XLA Modules:
  0.0 50.9 jit_solution(13960096966666834460)
XLA Ops:
  0.6 47.7 %laplace.1 = (f32[16,15,32,128]{3,2,1,0:T(8,128)S(1)}, f32[2,16,16]{2,1,0:T(8,128)}) custom-call(f32[16,12,32,128]{3,2,1,0:T(8,128)} %fiedler.1, s32[12,32,128]{2,1,0:T(8,128)} %labels.1), custom_call_target="tpu_custom_call" | custom-call | tf_op jit(solution)/shard_map/laplace/pallas_call | solution.py:478
  48.4 0.0 copy-start
  48.4 1.9 %copy.6 = f32[16,15,32,128]{3,2,1,0:T(8,128)} copy(f32[16,15,32,128]{3,2,1,0:T(8,128)S(1)} %get-tuple-element.2) | data formatting | bytes 7864320
  50.3 0.0 copy-done
  50.3 0.6 %copy.7 = f32[2,16,16]{2,1,0:T(8,128)} copy(f32[2,16,16]{2,1,0:T(8,128)S(1)} %copy-done) | data formatting | bytes 4096
Async XLA Ops:
  48.4 1.9 %copy-start = (f32[2,16,16]{2,1,0:T(8,128)S(1)}, f32[2,16,16]{2,1,0:T(8,128)}, u32[]{:S(2)}) copy-start(f32[2,16,16]{2,1,0:T(8,128)} %get-tuple-element.7) | copy-start | bytes 6148

commit v4 on v3

--- a/solution.py
+++ b/solution.py
@@ -8,8 +8,9 @@
 from jax.sharding import PartitionSpec as P
 
 REACH = 2
-EARLY_PLANES = 3
+EARLY_PLANES = 4
 CHUNKS = 3
+STORES = 4
 MESH = pl.DeviceIdType.MESH
 
 
@@ -99,6 +100,14 @@
             if dc or dl:
                 pl.semaphore_signal(barrier, inc=1, device_id=(lax.rem(c + dc, chain), lax.rem(l + dl, lanes)),
                                     device_id_type=MESH)
+    load_label.wait()
+    totals = [jnp.zeros((lines, width), jnp.float32) for _ in range(2)]
+    for p in range(planes):
+        here = label[p, 0:lines]
+        totals[0] += jnp.where((here == up_side) & (p >= planes - up_count), 1.0, 0.0)
+        totals[1] += jnp.where((here == down_side) & (p < down_count), 1.0, 0.0)
+    for way in range(2):
+        count[way] = totals[way]
     pl.semaphore_wait(barrier, chain * lanes - 1)
 
     lab_copies = [
@@ -159,6 +168,19 @@
                     for copy in corner_copies(way, j):
                         copy.start()
 
+    def count_copies(way):
+        to = (up_c, down_c)[way]
+        return [
+            remote(count.at[way], counted.at[way, 0:lines], cnt_s.at[way, 0], cnt_r.at[way, 0], (to, l)),
+            remote(count.at[way, lo], counted.at[way, nxt], cnt_s.at[way, 1], cnt_r.at[way, 1], (to, down_l)),
+            remote(count.at[way, hi], counted.at[way, prv], cnt_s.at[way, 2], cnt_r.at[way, 2], (to, up_l)),
+        ]
+
+    for way, total, _ in sends:
+        @pl.when(total > 0)
+        def _():
+            for copy in count_copies(way):
+                copy.start()
     for copy in lab_copies:
         copy.start()
     send_plane(1, False)
@@ -168,25 +190,8 @@
     for j in range(2, most + 1):
         send_plane(j, False)
 
-    load_label.wait()
     for copy in lab_copies:
         copy.wait_recv()
-
-    def count_copy(way):
-        return remote(count.at[way], counted.at[way], cnt_s.at[way], cnt_r.at[way], ((up_c, down_c)[way], l))
-
-    totals = [jnp.zeros((tall, width), jnp.float32) for _ in range(2)]
-    for p in range(planes):
-        here = label[p]
-        totals[0] += jnp.where((here == up_side) & (p >= planes - up_count), 1.0, 0.0)
-        totals[1] += jnp.where((here == down_side) & (p < down_count), 1.0, 0.0)
-    for way, total in ((0, up_count), (1, down_count)):
-        count[way] = totals[way]
-
-        @pl.when(total > 0)
-        def _():
-            count_copy(way).start()
-
     acc[...] = jnp.zeros(acc.shape, jnp.float32)
     for p in range(planes):
         mark[base + p] = jnp.where(label[p] == side, 1.0, 0.0)
@@ -372,7 +377,8 @@
             for way, total in ((0, below), (1, above)):
                 @pl.when(total > 0)
                 def _():
-                    count_copy(way).wait_recv()
+                    for copy in count_copies(way):
+                        copy.wait_recv()
         if i == ready:
             end_gram()
 
@@ -450,7 +456,8 @@
     for way, total, across in sends:
         @pl.when(total > 0)
         def _():
-            count_copy(way).wait_send()
+            for copy in count_copies(way):
+                copy.wait_send()
         for j in range(1, most + 1):
             @pl.when(j <= total)
             def _():
@@ -465,6 +472,18 @@
         def _():
             for copy in pass_copies(j):
                 copy.wait_send()
+
+
+def store_kernel(image, gram, image_out, gram_out, sems):
+    part = image.shape[0] // STORES
+    copies = [pltpu.make_async_copy(gram, gram_out, sems.at[STORES])]
+    for i in range(STORES):
+        rows = pl.ds(i * part, part)
+        copies.append(pltpu.make_async_copy(image.at[rows], image_out.at[rows], sems.at[i]))
+    for copy in copies:
+        copy.start()
+    for copy in copies:
+        copy.wait()
 
 
 def per_device(fiedler, side_labels):
@@ -475,13 +494,13 @@
     tall, frames, most = lines + 8, plan.frames, plan.most
     f32, dma = jnp.float32, pltpu.SemaphoreType.DMA
     anywhere, vmem = pl.BlockSpec(memory_space=pl.ANY), pl.BlockSpec(memory_space=pltpu.VMEM)
-    return pl.pallas_call(
+    image, gram = pl.pallas_call(
         functools.partial(kernel, plan, float(slots)),
         in_specs=[anywhere, anywhere],
         out_specs=[vmem, vmem],
         out_shape=[
             pltpu.VMEM((vectors, plan.band, lines, width), f32),
-            jax.ShapeDtypeStruct((2, vectors, vectors), f32),
+            pltpu.VMEM((2, vectors, vectors), f32),
         ],
         scratch_shapes=[
             pltpu.VMEM((vectors, frames, tall, width), f32),
@@ -489,7 +508,7 @@
             pltpu.VMEM((vectors, frames, tall, width), f32),
             pltpu.VMEM((frames, tall, width), f32),
             pltpu.VMEM((planes, tall, width), jnp.int32),
-            pltpu.VMEM((2, tall, width), f32),
+            pltpu.VMEM((2, lines, width), f32),
             pltpu.VMEM((2, tall, width), f32),
             pltpu.VMEM((vectors, lines, width), f32),
             pltpu.VMEM((2, 2, 8 * vectors, 8 * vectors), f32),
@@ -497,12 +516,21 @@
             pltpu.VMEM((chain * lanes, 8, width), f32),
             dma((2,)), dma((2,)), dma((2,)), dma((CHUNKS, 2)), dma((CHUNKS, 2)),
             dma((2, most)), dma((2, most)), dma((2, most, 2)), dma((2, most, 2)), dma((most, 2)),
-            dma((2,)), dma((2,)), dma((1,)), dma((1,)),
+            dma((2, 3)), dma((2, 3)), dma((1,)), dma((1,)),
         ],
         compiler_params=pltpu.CompilerParams(
             collective_id=0, has_side_effects=True, vmem_limit_bytes=56 * 1024 * 1024),
         name="laplace",
     )(fiedler, side_labels)
+    return pl.pallas_call(
+        store_kernel,
+        in_specs=[vmem, vmem],
+        out_specs=[anywhere, anywhere],
+        out_shape=[jax.ShapeDtypeStruct(a.shape, a.dtype) for a in (image, gram)],
+        scratch_shapes=[dma((STORES + 1,))],
+        compiler_params=pltpu.CompilerParams(vmem_limit_bytes=1024 * 1024),
+        name="store",
+    )(*(pltpu.with_memory_space_constraint(a, pltpu.VMEM) for a in (image, gram)))
 
 
 def solution(mesh):

time: 51.1 us -> 40.1 us (0.78)
  the two profiles are of different devices: /device:TPU:1 before, /device:TPU:2 now
where the time goes in v4:
time: 40.1 us; the launch traced here: 39.9 us
  Pallas kernels  39.3 us (98%)
  between operations  0.64 us (2%)
    pallas_call x1, Pallas kernels, per_device(): pl.pallas_call(functools.partial(kernel, plan, float(slots)), in_specs=[a...  37.3 us
    pallas_call x1, Pallas kernels, per_device(): pl.pallas_call(store_kernel, in_specs=[vmem, vmem], out_specs=[anywhere,...  1.97 us

profile of v4, /device:TPU:2, one launch (start us, length us, event | category | flops | bytes accessed | tf_op | source)
XLA Modules:
  0.0 39.9 jit_solution(9628647046464088587)
XLA Ops:
  0.6 37.3 %laplace.1 = (f32[16,15,32,128]{3,2,1,0:T(8,128)S(1)}, f32[2,16,16]{2,1,0:T(8,128)S(1)}) custom-call(f32[16,12,32,128]{3,2,1,0:T(8,128)} %fiedler.1, s32[12,32,128]{2,1,0:T(8,128)} %labels.1), custom_call_target="tpu_custom_call" | custom-call | tf_op jit(solution)/shard_map/laplace/pallas_call | solution.py:497
  38.0 2.0 %store.1 = (f32[16,15,32,128]{3,2,1,0:T(8,128)}, f32[2,16,16]{2,1,0:T(8,128)}) custom-call(f32[16,15,32,128]{3,2,1,0:T(8,128)S(1)} %get-tuple-element.4.image, f32[2,16,16]{2,1,0:T(8,128)S(1)} %get-tuple-element.5.gram), custom_call_target="tpu_custom_call" | custom-call | tf_op jit(solution)/shard_map/store/pallas_call | solution.py:525

commit v5 on v4

--- a/solution.py
+++ b/solution.py
@@ -8,8 +8,8 @@
 from jax.sharding import PartitionSpec as P
 
 REACH = 2
-EARLY_PLANES = 4
 CHUNKS = 3
+PARTS = 2
 STORES = 4
 MESH = pl.DeviceIdType.MESH
 
@@ -33,10 +33,11 @@
         spots = [self.spot(w, max_of=max) for w in range(self.half)]
         self.most = max(max(below, above) for _, below, above in spots)
         assert self.most <= planes and 8 * vectors == width
-        assert spots[0][1] == spots[-1][2] > 0 and spots[0][2] == spots[-1][1] == 0
+        assert spots[0][1] == spots[-1][2] > 4 and spots[0][2] == spots[-1][1] == 0
         self.end_near = spots[0][1]
+        self.most_far = max(min(below, above) for _, below, above in spots)
         self.chunk = planes // CHUNKS
-        assert self.chunk * CHUNKS == planes and self.chunk > 2
+        assert self.chunk * CHUNKS == planes and self.chunk > 2 and vectors % PARTS == 0
         self.pad = 1 + max(max(0, -slot) for slot, _, _ in spots)
         tail = 1 + max(max(0, slot + planes - self.window) for slot, _, _ in spots)
         self.frames = self.pad + self.window + tail
@@ -50,6 +51,10 @@
         above = max_of(0, self.window - REACH * last - slot - self.planes)
         return slot, below, above
 
+    def is_end(self, c):
+        within = self.place(c)[1]
+        return (within == 0) | (within == self.half - 1)
+
     def place(self, c):
         relative = lax.rem(c + (self.chain - self.chain // 4), self.chain)
         side = lax.div(relative, self.half)
@@ -58,8 +63,8 @@
 
 
 def kernel(plan, scale_of, fiedler, labels, image, gram, field, moved, once, mark, label, count, counted, spare, acc,
-           packed, got, local_sem, lab_s, lab_r, own_s, own_r, plane_s, plane_r, edge_s, edge_r, pass_s, cnt_s, cnt_r,
-           gram_s, gram_r):
+           weight, packed, handed, got, local_sem, lab_s, lab_r, own_s, own_r, plane_s, plane_r, last_s, last_r, edge_s, edge_r, pass_s, cnt_s, cnt_r,
+           hand_s, hand_r, gram_s, gram_r):
     chain, lanes, vectors, planes, lines, width = (
         plan.chain, plan.lanes, plan.vectors, plan.planes, plan.lines, plan.width)
     window, pad, most = plan.window, plan.pad, plan.most
@@ -111,37 +116,46 @@
     pl.semaphore_wait(barrier, chain * lanes - 1)
 
     lab_copies = [
-        remote(labels.at[:, lo], label.at[:, nxt], lab_s.at[0], lab_r.at[0], (c, down_l)),
-        remote(labels.at[:, hi], label.at[:, prv], lab_s.at[1], lab_r.at[1], (c, up_l)),
+        remote(label.at[:, lo], label.at[:, nxt], lab_s.at[0], lab_r.at[0], (c, down_l)),
+        remote(label.at[:, hi], label.at[:, prv], lab_s.at[1], lab_r.at[1], (c, up_l)),
     ]
     chunk = plan.chunk
 
     def own_copies(i):
         start = jnp.where(lower, i * chunk, planes - (i + 1) * chunk)
-        source, at = pl.ds(start, chunk), pl.ds(base + start, chunk)
+        at = pl.ds(base + start, chunk)
         return [
-            remote(fiedler.at[:, source, lo], field.at[:, at, nxt], own_s.at[i, 0], own_r.at[i, 0], (c, down_l)),
-            remote(fiedler.at[:, source, hi], field.at[:, at, prv], own_s.at[i, 1], own_r.at[i, 1], (c, up_l)),
+            remote(field.at[:, at, lo], field.at[:, at, nxt], own_s.at[i, 0], own_r.at[i, 0], (c, down_l)),
+            remote(field.at[:, at, hi], field.at[:, at, prv], own_s.at[i, 1], own_r.at[i, 1], (c, up_l)),
         ]
 
     sends = ((0, up_count, up_side != side), (1, down_count, down_side != side))
 
     def spot_of(way, j):
         if way == 0:
-            return planes - j, pad + up_slot - j, up_c
-        return j - 1, pad + down_slot + planes - 1 + j, down_c
+            return base + planes - j, pad + up_slot - j, up_c
+        return base + j - 1, pad + down_slot + planes - 1 + j, down_c
 
     def plane_copy(way, j):
         source, at, to = spot_of(way, j)
         return remote(
-            fiedler.at[:, source], field.at[:, at, 0:lines], plane_s.at[way, j - 1], plane_r.at[way, j - 1], (to, l))
+            field.at[:, source, 0:lines], field.at[:, at, 0:lines], plane_s.at[way, j - 1], plane_r.at[way, j - 1], (to, l))
+
+    def part_copies(way, j):
+        source, at, to = spot_of(way, j)
+        share = vectors // PARTS
+        return [
+            remote(field.at[i * share : (i + 1) * share, source, 0:lines],
+                   field.at[i * share : (i + 1) * share, at, 0:lines], last_s.at[way, i], last_r.at[way, i], (to, l))
+            for i in range(PARTS)
+        ]
 
     def corner_copies(way, j):
         source, at, to = spot_of(way, j)
         return [
-            remote(fiedler.at[:, source, lo], field.at[:, at, nxt], edge_s.at[way, j - 1, 0],
+            remote(field.at[:, source, lo], field.at[:, at, nxt], edge_s.at[way, j - 1, 0],
                    edge_r.at[way, j - 1, 0], (to, down_l)),
-            remote(fiedler.at[:, source, hi], field.at[:, at, prv], edge_s.at[way, j - 1, 1],
+            remote(field.at[:, source, hi], field.at[:, at, prv], edge_s.at[way, j - 1, 1],
                    edge_r.at[way, j - 1, 1], (to, up_l)),
         ]
 
@@ -157,16 +171,24 @@
                    (c, up_l)),
         ]
 
-    def send_plane(j, late):
+    def each_send(j, act):
         for way, total, across in sends:
-            @pl.when((j <= total) & (across if late else (jnp.logical_not(across) | (j <= EARLY_PLANES))))
+            @pl.when((j <= total) & jnp.logical_not(across & passed_on(j, total)))
             def _():
-                plane_copy(way, j).start()
-
-                @pl.when(jnp.logical_not(across & passed_on(j, total)))
-                def _():
-                    for copy in corner_copies(way, j):
-                        copy.start()
+                for copy in corner_copies(way, j):
+                    act(copy)
+
+            @pl.when((j < total) | ((j == total) & jnp.logical_not(across)))
+            def _():
+                act(plane_copy(way, j))
+
+            @pl.when((j == total) & across)
+            def _():
+                for copy in part_copies(way, j):
+                    act(copy)
+
+    def send_plane(j):
+        each_send(j, lambda copy: copy.start())
 
     def count_copies(way):
         to = (up_c, down_c)[way]
@@ -176,6 +198,7 @@
             remote(count.at[way, hi], counted.at[way, prv], cnt_s.at[way, 2], cnt_r.at[way, 2], (to, up_l)),
         ]
 
+    load_field.wait()
     for way, total, _ in sends:
         @pl.when(total > 0)
         def _():
@@ -183,12 +206,12 @@
                 copy.start()
     for copy in lab_copies:
         copy.start()
-    send_plane(1, False)
+    send_plane(1)
     for i in range(CHUNKS):
         for copy in own_copies(i):
             copy.start()
     for j in range(2, most + 1):
-        send_plane(j, False)
+        send_plane(j)
 
     for copy in lab_copies:
         copy.wait_recv()
@@ -198,15 +221,7 @@
 
     @pl.when(is_end)
     def _():
-        at = near_edge + d * (near + 1)
-        mark[at] = jnp.zeros((tall, width), jnp.float32)
-
-        def clear(k, _):
-            moved[k, at] = jnp.zeros((tall, width), jnp.float32)
-            once[k, at] = jnp.zeros((tall, width), jnp.float32)
-            return 0
-
-        lax.fori_loop(0, vectors, clear, 0)
+        mark[near_edge + d * (near + 1)] = jnp.zeros((tall, width), jnp.float32)
 
     def take(at):
         keep = mark[at] > 0.5
@@ -244,9 +259,9 @@
         def _():
             lax.fori_loop(0, vectors, one, 0, unroll=vectors)
 
-    def add_gram(read, which):
+    def add_gram(reads, which):
         block = jnp.concatenate(
-            [read(g).reshape(8 * vectors, width) for g in range(lines // 8)], axis=1)
+            [read(g).reshape(8 * vectors, width) for read in reads for g in range(lines // 8)], axis=1)
         high = block.astype(jnp.bfloat16)
         low = (block - high.astype(jnp.float32)).astype(jnp.bfloat16)
         dot = functools.partial(
@@ -254,8 +269,14 @@
         acc[which, 0] += dot(high, high)
         acc[which, 1] += dot(high, low)
 
-    def gram_of(s):
-        add_gram(lambda g: once[:, s, 8 * g : 8 * g + 8, :], 0)
+    def gram_of(spots):
+        def reader(s, counts):
+            def read(g):
+                return jnp.where(counts & in_band(s), once[:, s, 8 * g : 8 * g + 8, :], 0.0)
+
+            return read
+
+        add_gram([reader(s, counts) for s, counts in spots], 0)
 
     def in_band(s):
         return (s >= pad + REACH) & (s < pad + window - REACH)
@@ -270,40 +291,61 @@
         remote(fiedler.at[:, 0, hi], field.at[:, at, prv], edge_s.at[way, j - 1, 1], edge_r.at[way, j - 1, 1],
                (c, l)).wait_recv()
 
+    def near_mark(j):
+        at = near_edge + d * j
+        wait_edges(near_way, j, at)
+        mark[at] = jnp.where(counted[near_way] >= (j + 0.0) - 0.5, 1.0, 0.0)
+
     def near_use(j, _):
         at = near_edge + d * j
-
-        @pl.when(j <= near)
-        def _():
-            wait_edges(near_way, j, at)
-            mark[at] = jnp.where(counted[near_way] >= j.astype(jnp.float32) - 0.5, 1.0, 0.0)
-            take(at)
-
-        @pl.when(j <= near + 1)
-        def _():
-            apply_once(at - d)
-
-        @pl.when(in_band(at - d) & (jnp.logical_not(is_end) | (j == 1)))
-        def _():
-            gram_of(at - d)
-
+        near_mark(j)
+        take(at)
+        apply_once(at - d)
         apply_twice(at - 2 * d)
         return 0
 
-    def near_step(j, _):
-        goes_on = is_end & passed_on(j, near)
-
-        @pl.when(j <= near)
-        def _():
-            wait_plane(near_way, j, near_edge + d * j)
-
-        @pl.when(goes_on)
+    def last_use():
+        at = near_edge + d * near
+        near_mark(near)
+        for i in range(3):
+            s = at - d * i
+            degree, scale = weights(mark[s - 1], mark[s], mark[s + 1])
+            weight[i, 0], weight[i, 1] = degree, scale
+
+        def step(i, here, beside):
+            return weight[i, 0] * here - weight[i, 1] * (beside + two_sided(here))
+
+        def one(k, _):
+            moved_0 = jnp.where(mark[at] > 0.5, field[k, at], 0.0)
+            moved_1 = moved[k, at - d]
+            once_0 = step(0, moved_0, moved_1)
+            once_1 = step(1, moved_1, moved_0 + moved[k, at - 2 * d])
+            once_2 = once[k, at - 2 * d]
+            values = (
+                step(0, once_0, once_1), step(1, once_1, once_0 + once_2),
+                step(2, once_2, once_1 + once[k, at - 3 * d]))
+            for i in range(3):
+                image[k, at - d * i - pad - REACH] = values[i][0:lines]
+            return 0
+
+        share = vectors // PARTS
+        for i in range(PARTS):
+            part = field.at[i * share : (i + 1) * share, at, 0:lines]
+            remote(part, part, last_s.at[near_way, i], last_r.at[near_way, i], (c, l)).wait_recv()
+            lax.fori_loop(i * share, (i + 1) * share, one, 0, unroll=share)
+
+    def arrive(j):
+        wait_plane(near_way, j, near_edge + d * j)
+
+        @pl.when(is_end & passed_on(j, near))
         def _():
             for copy in pass_copies(j):
                 copy.start()
 
+    def near_step(j, _):
+        arrive(j)
         begin = jnp.where(is_end & passed_on(j - 1, near), j - 1, j)
-        lax.fori_loop(begin, jnp.where(goes_on, j, j + 1), near_use, 0)
+        lax.fori_loop(begin, jnp.where(is_end & passed_on(j, near), j, j + 1), near_use, 0)
         return 0
 
     def far_step(j, _):
@@ -314,10 +356,6 @@
         take(at)
         apply_once(at + d)
 
-        @pl.when(in_band(at + d))
-        def _():
-            gram_of(at + d)
-
         apply_twice(at + 2 * d)
         return 0
 
@@ -333,11 +371,10 @@
 
             value = part(here, at)
             value = degree * value - scale * (part(toward, at + d) + part(away, at - d) + two_sided(value))
-            spare[k] = value[0:lines]
+            spare[k, j - 1] = value[0:lines]
             return 0
 
         lax.fori_loop(0, vectors, one, 0, unroll=vectors)
-        add_gram(lambda g: spare[:, 8 * g : 8 * g + 8, :], 1)
         return 0
 
     def take_own(m, _):
@@ -350,10 +387,6 @@
         @pl.when((s > pad) & (s < pad + window - 1))
         def _():
             apply_once(s)
-
-        @pl.when(in_band(s))
-        def _():
-            gram_of(s)
         return 0
 
     def inner_twice(m, _):
@@ -365,14 +398,16 @@
         def _():
             lax.fori_loop(1, 2, near_step, 0)
             lax.fori_loop(1, near + 1, other_step, 0)
-
-    load_field.wait()
+            add_gram([lambda g, p=p: spare[:, p, 8 * g : 8 * g + 8, :] for p in range(plan.end_near)], 1)
+
     ready = min(CHUNKS - 1, plan.end_near // chunk)
     for i in range(CHUNKS):
         for copy in own_copies(i):
             copy.wait_recv()
         lax.fori_loop(i * chunk, (i + 1) * chunk, take_own, 0)
-        lax.fori_loop(max(1, i * chunk - 1), (i + 1) * chunk - 1, inner_once, 0)
+        inner = max(1, i * chunk - 1), (i + 1) * chunk - 1
+        lax.fori_loop(*inner, inner_once, 0)
+        gram_of([(near_edge - d * m, True) for m in range(*inner)])
         if i == 0:
             for way, total in ((0, below), (1, above)):
                 @pl.when(total > 0)
@@ -382,54 +417,85 @@
         if i == ready:
             end_gram()
 
+            @pl.when(is_end)
+            def _():
+                arrive(2)
+
     @pl.when(jnp.logical_not(is_end))
     def _():
-        lax.fori_loop(2, planes - 2, inner_twice, 0)
         lax.fori_loop(1, near + 1, near_step, 0)
+        gram_of([(near_edge + d * (j - 1), j <= near) for j in range(1, most + 1)])
 
     lax.fori_loop(1, far + 1, far_step, 0)
-
-    me = c * lanes + l
+    gram_of([(near_edge, is_end)] + [(far_edge - d * (j - 1), j <= far) for j in range(1, plan.most_far + 1)])
+
     lane_of = functools.partial(lax.broadcasted_iota, jnp.int32)
+    ones = jnp.where(lax.div(lane_of((width, width), 0), 8) == lax.div(lane_of((width, width), 1), 8), 1.0, 0.0)
+    pick = lane_of((8, width), 0) == lax.rem(lane_of((8, width), 1), 8)
+    shape = (vectors, 8, width)
+    diagonal = lane_of(shape, 1) == lax.rem(lane_of(shape, 2), 8)
+    rows = []
     for which in range(2):
         total = acc[which, 0] + (acc[which, 1] + acc[which, 1].T)
-        shape = (vectors, 8, width)
-        diagonal = lane_of(shape, 1) == lax.rem(lane_of(shape, 2), 8)
-        rows = jnp.sum(jnp.where(diagonal, total.reshape(shape), 0.0), axis=1)
-        ones = jnp.where(lax.div(lane_of((width, width), 0), 8) == lax.div(lane_of((width, width), 1), 8), 1.0, 0.0)
-        rows = jnp.dot(rows, ones, precision=lax.Precision.HIGHEST, preferred_element_type=jnp.float32)
-        half = (8, width)
-        pick = lane_of(half, 0) == lax.rem(lane_of(half, 1), 8)
-        for h in range(vectors // 8):
-            row = jnp.sum(jnp.where(pick, rows[8 * h : 8 * h + 8], 0.0), axis=0, keepdims=True)
-            for place in range(2):
-                @pl.when((side if which == 0 else 1 - side) == place)
-                def _():
-                    packed[place * (vectors // 8) + h : place * (vectors // 8) + h + 1, :] = row
-    count_rows = 2 * (vectors // 8)
+        rows.append(jnp.sum(jnp.where(diagonal, total.reshape(shape), 0.0), axis=1))
+    folded = jnp.dot(jnp.concatenate(rows, axis=0), ones, precision=lax.Precision.HIGHEST,
+                     preferred_element_type=jnp.float32)
+    parts = vectors // 8
+    terms = [jnp.sum(jnp.where(pick, folded[8 * h : 8 * h + 8], 0.0), axis=0, keepdims=True) for h in range(2 * parts)]
+    for h in range(parts):
+        packed[h : h + 1, :] = jnp.where(side == 0, terms[h], terms[parts + h])
+        packed[parts + h : parts + h + 1, :] = jnp.where(side == 0, terms[parts + h], terms[h])
+    count_rows = 2 * parts
     body = packed.at[0:count_rows]
-    for dc in range(chain):
-        for dl in range(lanes):
-            if dc or dl:
-                remote(body, got.at[me, 0:count_rows], gram_s.at[0], gram_r.at[0],
-                       (lax.rem(c + dc, chain), lax.rem(l + dl, lanes))).start()
-    got[me, 0:count_rows] = packed[0:count_rows]
-
-    for j in range(EARLY_PLANES + 1, most + 1):
-        send_plane(j, True)
+    chips = chain // 2 * lanes
+    slot_of = lax.div(c, 2) * lanes + l
+    partner = c + 1 - 2 * lax.rem(c, 2)
+    leads = jnp.logical_not(is_end) & (plan.is_end(partner) | (lax.rem(c, 2) == 0))
+    hand_over = remote(body, handed.at[0:count_rows], hand_s.at[0], hand_r.at[0], (partner, l))
+
+    def broadcast(dc, dl):
+        return remote(got.at[slot_of, 0:count_rows], got.at[slot_of, 0:count_rows], gram_s.at[0], gram_r.at[0],
+                      (lax.rem(c + dc, chain), lax.rem(l + dl, lanes)))
+
+    @pl.when(jnp.logical_not(leads))
+    def _():
+        hand_over.start()
+
+    @pl.when(leads)
+    def _():
+        hand_over.wait_recv()
+        got[slot_of, 0:count_rows] = packed[0:count_rows] + handed[0:count_rows]
+        for dc in range(chain):
+            for dl in range(lanes):
+                if dc or dl:
+                    broadcast(dc, dl).start()
 
     @pl.when(is_end)
     def _():
-        lax.fori_loop(2, planes - 2, inner_twice, 0)
-        lax.fori_loop(2, near, near_step, 0)
-
-    everyone = got.at[0 : chain * lanes - 1, 0:count_rows]
-    remote(everyone, everyone, gram_s.at[0], gram_r.at[0], (c, l)).wait_recv()
+        arrive(3)
+
+    lax.fori_loop(2, planes - 2, inner_twice, 0)
+
+    @pl.when(is_end)
+    def _():
+        lax.fori_loop(2, 3, near_use, 0)
+        lax.fori_loop(4, near, near_step, 0)
+
+    def many(total):
+        return remote(got.at[0:total, 0:count_rows], got.at[0:total, 0:count_rows], gram_s.at[0], gram_r.at[0], (c, l))
+
+    @pl.when(leads)
+    def _():
+        many(chips - 1).wait_recv()
+
+    @pl.when(jnp.logical_not(leads))
+    def _():
+        many(chips).wait_recv()
 
     def sum_one(i, total):
         return total + got[i, 0:count_rows]
 
-    total = lax.fori_loop(1, chain * lanes, sum_one, got[0, 0:count_rows], unroll=True)
+    total = lax.fori_loop(1, chips, sum_one, got[0, 0:count_rows], unroll=True)
     tall_shape = (vectors, width)
     inside = lax.div(lane_of(tall_shape, 1), 8) == lane_of(tall_shape, 0)
     choose = jnp.where(
@@ -443,35 +509,42 @@
             result = jnp.where(lax.div(lane_of(tall_shape, 1), 8) == h, spread, result)
         gram[place] = result[:, 0:vectors] / scale_of
 
-    @pl.when(is_end)
-    def _():
-        lax.fori_loop(near, near + 3, near_step, 0)
-
-    remote(everyone, everyone, gram_s.at[0], gram_r.at[0], (c, l)).wait_send()
+    def finish(copy):
+        copy.wait_send()
+
+    @pl.when(leads)
+    def _():
+        sent = got.at[0 : chain * lanes - 1, 0:count_rows]
+        remote(sent, sent, gram_s.at[0], gram_r.at[0], (c, l)).wait_send()
+
+    @pl.when(jnp.logical_not(leads))
+    def _():
+        hand_over.wait_send()
+
     for i in range(CHUNKS):
         for copy in own_copies(i):
             copy.wait_send()
     for copy in lab_copies:
         copy.wait_send()
-    for way, total, across in sends:
+    for way, total, _ in sends:
         @pl.when(total > 0)
         def _():
             for copy in count_copies(way):
                 copy.wait_send()
-        for j in range(1, most + 1):
-            @pl.when(j <= total)
-            def _():
-                plane_copy(way, j).wait_send()
-
-                @pl.when(jnp.logical_not(across & passed_on(j, total)))
-                def _():
-                    for copy in corner_copies(way, j):
-                        copy.wait_send()
     for j in range(1, most + 1):
         @pl.when(is_end & passed_on(j, near))
         def _():
             for copy in pass_copies(j):
                 copy.wait_send()
+    for j in range(1, most - 1):
+        each_send(j, finish)
+
+    @pl.when(is_end)
+    def _():
+        last_use()
+
+    for j in range(max(1, most - 1), most + 1):
+        each_send(j, finish)
 
 
 def store_kernel(image, gram, image_out, gram_out, sems):
@@ -510,13 +583,15 @@
             pltpu.VMEM((planes, tall, width), jnp.int32),
             pltpu.VMEM((2, lines, width), f32),
             pltpu.VMEM((2, tall, width), f32),
-            pltpu.VMEM((vectors, lines, width), f32),
+            pltpu.VMEM((vectors, plan.end_near, lines, width), f32),
             pltpu.VMEM((2, 2, 8 * vectors, 8 * vectors), f32),
+            pltpu.VMEM((3, 2, tall, width), f32),
+            pltpu.VMEM((8, width), f32),
             pltpu.VMEM((8, width), f32),
             pltpu.VMEM((chain * lanes, 8, width), f32),
             dma((2,)), dma((2,)), dma((2,)), dma((CHUNKS, 2)), dma((CHUNKS, 2)),
-            dma((2, most)), dma((2, most)), dma((2, most, 2)), dma((2, most, 2)), dma((most, 2)),
-            dma((2, 3)), dma((2, 3)), dma((1,)), dma((1,)),
+            dma((2, most)), dma((2, most)), dma((2, PARTS)), dma((2, PARTS)), dma((2, most, 2)), dma((2, most, 2)), dma((most, 2)),
+            dma((2, 3)), dma((2, 3)), dma((1,)), dma((1,)), dma((1,)), dma((1,)),
         ],
         compiler_params=pltpu.CompilerParams(
             collective_id=0, has_side_effects=True, vmem_limit_bytes=56 * 1024 * 1024),

time: 40.1 us -> 37.8 us (0.943)
  the two profiles are of different devices: /device:TPU:2 before, /device:TPU:1 now
where the time goes in v5:
time: 37.8 us; the launch traced here: 37.6 us
  Pallas kernels  37 us (98%)
  between operations  0.64 us (2%)
    pallas_call x1, Pallas kernels, per_device(): pl.pallas_call(functools.partial(kernel, plan, float(slots)), in_specs=[a...  35 us
    pallas_call x1, Pallas kernels, per_device(): pl.pallas_call(store_kernel, in_specs=[vmem, vmem], out_specs=[anywhere,...  1.97 us

profile of v5, /device:TPU:1, one launch (start us, length us, event | category | flops | bytes accessed | tf_op | source)
XLA Modules:
  0.0 37.6 jit_solution(1000985891248425966)
XLA Ops:
  0.6 35.0 %laplace.1 = (f32[16,15,32,128]{3,2,1,0:T(8,128)S(1)}, f32[2,16,16]{2,1,0:T(8,128)S(1)}) custom-call(f32[16,12,32,128]{3,2,1,0:T(8,128)} %fiedler.1, s32[12,32,128]{2,1,0:T(8,128)} %labels.1), custom_call_target="tpu_custom_call" | custom-call | tf_op jit(solution)/shard_map/laplace/pallas_call | solution.py:570
  35.7 2.0 %store.1 = (f32[16,15,32,128]{3,2,1,0:T(8,128)}, f32[2,16,16]{2,1,0:T(8,128)}) custom-call(f32[16,15,32,128]{3,2,1,0:T(8,128)S(1)} %get-tuple-element.4.image, f32[2,16,16]{2,1,0:T(8,128)S(1)} %get-tuple-element.5.gram), custom_call_target="tpu_custom_call" | custom-call | tf_op jit(solution)/shard_map/store/pallas_call | solution.py:600

commit v6 on v5

--- a/solution.py
+++ b/solution.py
@@ -36,6 +36,9 @@
         assert spots[0][1] == spots[-1][2] > 4 and spots[0][2] == spots[-1][1] == 0
         self.end_near = spots[0][1]
         self.most_far = max(min(below, above) for _, below, above in spots)
+        self.totals = sorted({count for _, below, above in spots for count in (below, above)} - {0})
+        self.rounds = chain // 2
+        assert self.rounds % 4 == 0 and lanes % 2 == 0 and lanes > 2
         self.chunk = planes // CHUNKS
         assert self.chunk * CHUNKS == planes and self.chunk > 2 and vectors % PARTS == 0
         self.pad = 1 + max(max(0, -slot) for slot, _, _ in spots)
@@ -63,8 +66,8 @@
 
 
 def kernel(plan, scale_of, fiedler, labels, image, gram, field, moved, once, mark, label, count, counted, spare, acc,
-           weight, packed, handed, got, local_sem, lab_s, lab_r, own_s, own_r, plane_s, plane_r, last_s, last_r, edge_s, edge_r, pass_s, cnt_s, cnt_r,
-           hand_s, hand_r, gram_s, gram_r):
+           weight, packed, handed, got, local_sem, lab_s, lab_r, own_s, own_r, plane_s, plane_r, last_r, corner_s, edge_r,
+           pass_s, cnt_s, cnt_r, hand_s, hand_r, gram_s, gram_r, lane_told, tell, cross, chain_told):
     chain, lanes, vectors, planes, lines, width = (
         plan.chain, plan.lanes, plan.vectors, plan.planes, plan.lines, plan.width)
     window, pad, most = plan.window, plan.pad, plan.most
@@ -100,11 +103,17 @@
     load_field.start()
 
     barrier = pltpu.get_barrier_semaphore()
-    for dc in range(chain):
-        for dl in range(lanes):
-            if dc or dl:
-                pl.semaphore_signal(barrier, inc=1, device_id=(lax.rem(c + dc, chain), lax.rem(l + dl, lanes)),
-                                    device_id_type=MESH)
+    def signal(sem, device):
+        pl.semaphore_signal(sem, inc=1, device_id=device, device_id_type=MESH)
+
+    signal(barrier, (up_c, l))
+    signal(barrier, (down_c, l))
+
+    @pl.when(jnp.logical_not(is_end))
+    def _():
+        signal(barrier, (c, up_l))
+        signal(barrier, (c, down_l))
+
     load_label.wait()
     totals = [jnp.zeros((lines, width), jnp.float32) for _ in range(2)]
     for p in range(planes):
@@ -113,11 +122,20 @@
         totals[1] += jnp.where((here == down_side) & (p < down_count), 1.0, 0.0)
     for way in range(2):
         count[way] = totals[way]
-    pl.semaphore_wait(barrier, chain * lanes - 1)
+
+    @pl.when(is_end)
+    def _():
+        pl.semaphore_wait(barrier, 2)
+
+    @pl.when(jnp.logical_not(is_end))
+    def _():
+        pl.semaphore_wait(barrier, 4)
+        signal(lane_told.at[0], (c, up_l))
+        signal(lane_told.at[0], (c, down_l))
 
     lab_copies = [
         remote(label.at[:, lo], label.at[:, nxt], lab_s.at[0], lab_r.at[0], (c, down_l)),
-        remote(label.at[:, hi], label.at[:, prv], lab_s.at[1], lab_r.at[1], (c, up_l)),
+        remote(label.at[:, hi], label.at[:, prv], lab_s.at[0], lab_r.at[0], (c, up_l)),
     ]
     chunk = plan.chunk
 
@@ -125,11 +143,14 @@
         start = jnp.where(lower, i * chunk, planes - (i + 1) * chunk)
         at = pl.ds(base + start, chunk)
         return [
-            remote(field.at[:, at, lo], field.at[:, at, nxt], own_s.at[i, 0], own_r.at[i, 0], (c, down_l)),
-            remote(field.at[:, at, hi], field.at[:, at, prv], own_s.at[i, 1], own_r.at[i, 1], (c, up_l)),
+            remote(field.at[:, at, lo], field.at[:, at, nxt], own_s.at[0], own_r.at[i], (c, down_l)),
+            remote(field.at[:, at, hi], field.at[:, at, prv], own_s.at[0], own_r.at[i], (c, up_l)),
         ]
 
     sends = ((0, up_count, up_side != side), (1, down_count, down_side != side))
+    up_near, down_near = up_within < plan.half // 2, down_within >= plan.half // 2
+    first_sem = (jnp.where(up_near, 0, most), jnp.where(down_near, 0, most))
+    count_sem = (jnp.where(up_near, 0, 1), jnp.where(down_near, 0, 1))
 
     def spot_of(way, j):
         if way == 0:
@@ -139,24 +160,25 @@
     def plane_copy(way, j):
         source, at, to = spot_of(way, j)
         return remote(
-            field.at[:, source, 0:lines], field.at[:, at, 0:lines], plane_s.at[way, j - 1], plane_r.at[way, j - 1], (to, l))
+            field.at[:, source, 0:lines], field.at[:, at, 0:lines], plane_s.at[way],
+            plane_r.at[first_sem[way] + j - 1], (to, l))
 
     def part_copies(way, j):
         source, at, to = spot_of(way, j)
         share = vectors // PARTS
         return [
             remote(field.at[i * share : (i + 1) * share, source, 0:lines],
-                   field.at[i * share : (i + 1) * share, at, 0:lines], last_s.at[way, i], last_r.at[way, i], (to, l))
+                   field.at[i * share : (i + 1) * share, at, 0:lines], plane_s.at[way], last_r.at[i], (to, l))
             for i in range(PARTS)
         ]
 
     def corner_copies(way, j):
         source, at, to = spot_of(way, j)
         return [
-            remote(field.at[:, source, lo], field.at[:, at, nxt], edge_s.at[way, j - 1, 0],
-                   edge_r.at[way, j - 1, 0], (to, down_l)),
-            remote(field.at[:, source, hi], field.at[:, at, prv], edge_s.at[way, j - 1, 1],
-                   edge_r.at[way, j - 1, 1], (to, up_l)),
+            remote(field.at[:, source, lo], field.at[:, at, nxt], corner_s.at[way],
+                   edge_r.at[first_sem[way] + j - 1], (to, down_l)),
+            remote(field.at[:, source, hi], field.at[:, at, prv], corner_s.at[way],
+                   edge_r.at[first_sem[way] + j - 1], (to, up_l)),
         ]
 
     def passed_on(j, total):
@@ -165,56 +187,116 @@
     def pass_copies(j):
         at = near_edge + d * j
         return [
-            remote(field.at[:, at, lo], field.at[:, at, nxt], pass_s.at[j - 1, 0], edge_r.at[near_way, j - 1, 0],
+            remote(field.at[:, at, lo], field.at[:, at, nxt], pass_s.at[0], edge_r.at[j - 1],
                    (c, down_l)),
-            remote(field.at[:, at, hi], field.at[:, at, prv], pass_s.at[j - 1, 1], edge_r.at[near_way, j - 1, 1],
+            remote(field.at[:, at, hi], field.at[:, at, prv], pass_s.at[0], edge_r.at[j - 1],
                    (c, up_l)),
         ]
 
-    def each_send(j, act):
+    def send_plane(j):
+        for way, total, across in sends:
+            @pl.when((j < total) | ((j == total) & jnp.logical_not(across)))
+            def _():
+                plane_copy(way, j).start()
+
+            @pl.when((j == total) & across)
+            def _():
+                for copy in part_copies(way, j):
+                    copy.start()
+
+    def send_corners(j):
         for way, total, across in sends:
             @pl.when((j <= total) & jnp.logical_not(across & passed_on(j, total)))
             def _():
                 for copy in corner_copies(way, j):
-                    act(copy)
-
-            @pl.when((j < total) | ((j == total) & jnp.logical_not(across)))
+                    copy.start()
+
+    def count_copies(way, corners):
+        to = (up_c, down_c)[way]
+        send, recv = cnt_s.at[way], cnt_r.at[count_sem[way]]
+        if not corners:
+            return [remote(count.at[way], counted.at[way, 0:lines], send, recv, (to, l))]
+        return [
+            remote(count.at[way, lo], counted.at[way, nxt], send, recv, (to, down_l)),
+            remote(count.at[way, hi], counted.at[way, prv], send, recv, (to, up_l)),
+        ]
+
+    def start_counts(corners):
+        for way, total, _ in sends:
+            @pl.when(total > 0)
             def _():
-                act(plane_copy(way, j))
-
-            @pl.when((j == total) & across)
-            def _():
-                for copy in part_copies(way, j):
-                    act(copy)
-
-    def send_plane(j):
-        each_send(j, lambda copy: copy.start())
-
-    def count_copies(way):
-        to = (up_c, down_c)[way]
-        return [
-            remote(count.at[way], counted.at[way, 0:lines], cnt_s.at[way, 0], cnt_r.at[way, 0], (to, l)),
-            remote(count.at[way, lo], counted.at[way, nxt], cnt_s.at[way, 1], cnt_r.at[way, 1], (to, down_l)),
-            remote(count.at[way, hi], counted.at[way, prv], cnt_s.at[way, 2], cnt_r.at[way, 2], (to, up_l)),
-        ]
+                for copy in count_copies(way, corners):
+                    copy.start()
+
+    partner = c + 1 - 2 * lax.rem(c, 2)
+    partner_end = plan.is_end(partner)
+    cross_c = lax.rem(c + d + chain, chain)
+
+    def start_lanes():
+        for copy in lab_copies:
+            copy.start()
+        for i in range(CHUNKS):
+            for copy in own_copies(i):
+                copy.start()
 
     load_field.wait()
-    for way, total, _ in sends:
-        @pl.when(total > 0)
+    start_counts(False)
+    send_plane(1)
+
+    @pl.when(is_end)
+    def _():
+        pl.semaphore_wait(tell.at[0], 1)
+        signal(cross.at[0], (cross_c, l))
+        start_lanes()
+        pl.semaphore_wait(cross.at[0], 1)
+
+    @pl.when(jnp.logical_not(is_end))
+    def _():
+        start_lanes()
+        pl.semaphore_wait(lane_told.at[0], 2)
+
+        @pl.when(partner_end)
         def _():
-            for copy in count_copies(way):
-                copy.start()
-    for copy in lab_copies:
-        copy.start()
-    send_plane(1)
-    for i in range(CHUNKS):
-        for copy in own_copies(i):
-            copy.start()
+            signal(tell.at[0], (partner, l))
+
+        signal(lane_told.at[1], (c, up_l))
+        signal(lane_told.at[1], (c, down_l))
+
+    start_counts(True)
+    send_corners(1)
     for j in range(2, most + 1):
+        send_corners(j)
         send_plane(j)
 
-    for copy in lab_copies:
-        copy.wait_recv()
+    @pl.when(jnp.logical_not(is_end))
+    def _():
+        for r in range(1, lanes // 2):
+            pl.semaphore_wait(lane_told.at[r], 2)
+            if r + 1 < lanes // 2:
+                signal(lane_told.at[r + 1], (c, up_l))
+                signal(lane_told.at[r + 1], (c, down_l))
+
+    def tell_chain(r):
+        signal(chain_told.at[r], (up_c, l))
+        signal(chain_told.at[r], (down_c, l))
+
+    def chain_rounds(point):
+        each = plan.rounds // 4
+        for r in range(point * each, (point + 1) * each):
+            pl.semaphore_wait(chain_told.at[r], 2)
+            if r + 1 < plan.rounds:
+                tell_chain(r + 1)
+
+    tell_chain(0)
+
+    def drain(ref, recv):
+        remote(ref, ref, lab_s.at[0], recv, (c, l)).wait_recv()
+
+    def flush(ref, send):
+        remote(ref, ref, send, lab_r.at[0], (c, l)).wait_send()
+
+    both = slice(0, 2 * REACH)
+    drain(label.at[:, both], lab_r.at[0])
     acc[...] = jnp.zeros(acc.shape, jnp.float32)
     for p in range(planes):
         mark[base + p] = jnp.where(label[p] == side, 1.0, 0.0)
@@ -281,19 +363,15 @@
     def in_band(s):
         return (s >= pad + REACH) & (s < pad + window - REACH)
 
-    def wait_plane(way, j, at):
-        remote(fiedler.at[:, 0], field.at[:, at, 0:lines], plane_s.at[way, j - 1], plane_r.at[way, j - 1],
-               (c, l)).wait_recv()
-
-    def wait_edges(way, j, at):
-        remote(fiedler.at[:, 0, lo], field.at[:, at, nxt], edge_s.at[way, j - 1, 0], edge_r.at[way, j - 1, 0],
-               (c, l)).wait_recv()
-        remote(fiedler.at[:, 0, hi], field.at[:, at, prv], edge_s.at[way, j - 1, 1], edge_r.at[way, j - 1, 1],
-               (c, l)).wait_recv()
+    def wait_plane(index, at):
+        drain(field.at[:, at, 0:lines], plane_r.at[index])
+
+    def wait_edges(index, at):
+        drain(field.at[:, at, both], edge_r.at[index])
 
     def near_mark(j):
         at = near_edge + d * j
-        wait_edges(near_way, j, at)
+        wait_edges(j - 1, at)
         mark[at] = jnp.where(counted[near_way] >= (j + 0.0) - 0.5, 1.0, 0.0)
 
     def near_use(j, _):
@@ -330,12 +408,11 @@
 
         share = vectors // PARTS
         for i in range(PARTS):
-            part = field.at[i * share : (i + 1) * share, at, 0:lines]
-            remote(part, part, last_s.at[near_way, i], last_r.at[near_way, i], (c, l)).wait_recv()
+            drain(field.at[i * share : (i + 1) * share, at, 0:lines], last_r.at[i])
             lax.fori_loop(i * share, (i + 1) * share, one, 0, unroll=share)
 
     def arrive(j):
-        wait_plane(near_way, j, near_edge + d * j)
+        wait_plane(j - 1, near_edge + d * j)
 
         @pl.when(is_end & passed_on(j, near))
         def _():
@@ -350,8 +427,8 @@
 
     def far_step(j, _):
         at = far_edge - d * j
-        wait_plane(far_way, j, at)
-        wait_edges(far_way, j, at)
+        wait_plane(most + j - 1, at)
+        wait_edges(most + j - 1, at)
         mark[at] = jnp.where(counted[far_way] >= (far - j + 1).astype(jnp.float32) - 0.5, 1.0, 0.0)
         take(at)
         apply_once(at + d)
@@ -402,19 +479,17 @@
 
     ready = min(CHUNKS - 1, plan.end_near // chunk)
     for i in range(CHUNKS):
-        for copy in own_copies(i):
-            copy.wait_recv()
+        drain(field.at[:, 0:chunk, both], own_r.at[i])
+        chain_rounds(i)
         lax.fori_loop(i * chunk, (i + 1) * chunk, take_own, 0)
         inner = max(1, i * chunk - 1), (i + 1) * chunk - 1
         lax.fori_loop(*inner, inner_once, 0)
         gram_of([(near_edge - d * m, True) for m in range(*inner)])
-        if i == 0:
-            for way, total in ((0, below), (1, above)):
+        if i == ready:
+            for way, total in ((near_way, near), (far_way, far)):
                 @pl.when(total > 0)
                 def _():
-                    for copy in count_copies(way):
-                        copy.wait_recv()
-        if i == ready:
+                    drain(counted.at[way, 0 : lines + 2 * REACH], cnt_r.at[0 if way is near_way else 1])
             end_gram()
 
             @pl.when(is_end)
@@ -449,8 +524,7 @@
     body = packed.at[0:count_rows]
     chips = chain // 2 * lanes
     slot_of = lax.div(c, 2) * lanes + l
-    partner = c + 1 - 2 * lax.rem(c, 2)
-    leads = jnp.logical_not(is_end) & (plan.is_end(partner) | (lax.rem(c, 2) == 0))
+    leads = jnp.logical_not(is_end) & (partner_end | (lax.rem(c, 2) == 0))
     hand_over = remote(body, handed.at[0:count_rows], hand_s.at[0], hand_r.at[0], (partner, l))
 
     def broadcast(dc, dl):
@@ -463,6 +537,7 @@
 
     @pl.when(leads)
     def _():
+        chain_rounds(3)
         hand_over.wait_recv()
         got[slot_of, 0:count_rows] = packed[0:count_rows] + handed[0:count_rows]
         for dc in range(chain):
@@ -490,6 +565,7 @@
 
     @pl.when(jnp.logical_not(leads))
     def _():
+        chain_rounds(3)
         many(chips).wait_recv()
 
     def sum_one(i, total):
@@ -509,9 +585,6 @@
             result = jnp.where(lax.div(lane_of(tall_shape, 1), 8) == h, spread, result)
         gram[place] = result[:, 0:vectors] / scale_of
 
-    def finish(copy):
-        copy.wait_send()
-
     @pl.when(leads)
     def _():
         sent = got.at[0 : chain * lanes - 1, 0:count_rows]
@@ -521,30 +594,31 @@
     def _():
         hand_over.wait_send()
 
-    for i in range(CHUNKS):
-        for copy in own_copies(i):
-            copy.wait_send()
-    for copy in lab_copies:
-        copy.wait_send()
-    for way, total, _ in sends:
+    flush(field.at[:, 0:planes, both], own_s.at[0])
+    flush(label.at[:, both], lab_s.at[0])
+
+    @pl.when(is_end)
+    def _():
+        flush(field.at[:, 0 : plan.end_near - 3, both], pass_s.at[0])
+        last_use()
+
+    for way, total, across in sends:
         @pl.when(total > 0)
         def _():
-            for copy in count_copies(way):
-                copy.wait_send()
-    for j in range(1, most + 1):
-        @pl.when(is_end & passed_on(j, near))
+            flush(counted.at[way, 0 : lines + 2 * REACH], cnt_s.at[way])
+
+        @pl.when(across)
         def _():
-            for copy in pass_copies(j):
-                copy.wait_send()
-    for j in range(1, most - 1):
-        each_send(j, finish)
-
-    @pl.when(is_end)
-    def _():
-        last_use()
-
-    for j in range(max(1, most - 1), most + 1):
-        each_send(j, finish)
+            flush(field.at[:, 0:3, both], corner_s.at[way])
+
+        for t in plan.totals:
+            @pl.when(total == t)
+            def _():
+                flush(field.at[:, 0:t, 0:lines], plane_s.at[way])
+
+            @pl.when((total == t) & jnp.logical_not(across))
+            def _():
+                flush(field.at[:, 0:t, both], corner_s.at[way])
 
 
 def store_kernel(image, gram, image_out, gram_out, sems):
@@ -565,7 +639,7 @@
     plan = Plan(chain, lanes, vectors, planes, lines, width)
     slots = plan.band * plan.half * lines * lanes * width
     tall, frames, most = lines + 8, plan.frames, plan.most
-    f32, dma = jnp.float32, pltpu.SemaphoreType.DMA
+    f32, dma, regular = jnp.float32, pltpu.SemaphoreType.DMA, pltpu.SemaphoreType.REGULAR
     anywhere, vmem = pl.BlockSpec(memory_space=pl.ANY), pl.BlockSpec(memory_space=pltpu.VMEM)
     image, gram = pl.pallas_call(
         functools.partial(kernel, plan, float(slots)),
@@ -589,9 +663,10 @@
             pltpu.VMEM((8, width), f32),
             pltpu.VMEM((8, width), f32),
             pltpu.VMEM((chain * lanes, 8, width), f32),
-            dma((2,)), dma((2,)), dma((2,)), dma((CHUNKS, 2)), dma((CHUNKS, 2)),
-            dma((2, most)), dma((2, most)), dma((2, PARTS)), dma((2, PARTS)), dma((2, most, 2)), dma((2, most, 2)), dma((most, 2)),
-            dma((2, 3)), dma((2, 3)), dma((1,)), dma((1,)), dma((1,)), dma((1,)),
+            dma((2,)), dma((1,)), dma((1,)), dma((1,)), dma((CHUNKS,)),
+            dma((2,)), dma((most + plan.most_far,)), dma((PARTS,)), dma((2,)), dma((most + plan.most_far,)),
+            dma((1,)), dma((2,)), dma((2,)), dma((1,)), dma((1,)), dma((1,)), dma((1,)),
+            regular((lanes // 2,)), regular((1,)), regular((1,)), regular((plan.rounds,)),
         ],
         compiler_params=pltpu.CompilerParams(
             collective_id=0, has_side_effects=True, vmem_limit_bytes=56 * 1024 * 1024),

time: 37.8 us -> 35.4 us (0.937)
  Pallas kernels: 37 us -> 34.7 us
    pallas_call x1, Pallas kernels: 35 us -> 32.7 us  [per_device(): pl.pallas_call(functools.partial(kernel, plan, float(slots)), in_specs=[a...]
where the time goes in v6:
time: 35.4 us; the launch traced here: 35.3 us
  Pallas kernels  34.7 us (98%)
  between operations  0.64 us (2%)
    pallas_call x1, Pallas kernels, per_device(): pl.pallas_call(functools.partial(kernel, plan, float(slots)), in_specs=[a...  32.7 us
    pallas_call x1, Pallas kernels, per_device(): pl.pallas_call(store_kernel, in_specs=[vmem, vmem], out_specs=[anywhere,...  1.97 us

profile of v6, /device:TPU:1, one launch (start us, length us, event | category | flops | bytes accessed | tf_op | source)
XLA Modules:
  0.0 35.3 jit_solution(1440391786435346611)
XLA Ops:
  0.6 32.7 %laplace.1 = (f32[16,15,32,128]{3,2,1,0:T(8,128)S(1)}, f32[2,16,16]{2,1,0:T(8,128)S(1)}) custom-call(f32[16,12,32,128]{3,2,1,0:T(8,128)} %fiedler.1, s32[12,32,128]{2,1,0:T(8,128)} %labels.1), custom_call_target="tpu_custom_call" | custom-call | tf_op jit(solution)/shard_map/laplace/pallas_call | solution.py:644
  33.3 2.0 %store.1 = (f32[16,15,32,128]{3,2,1,0:T(8,128)}, f32[2,16,16]{2,1,0:T(8,128)}) custom-call(f32[16,15,32,128]{3,2,1,0:T(8,128)S(1)} %get-tuple-element.4.image, f32[2,16,16]{2,1,0:T(8,128)S(1)} %get-tuple-element.5.gram), custom_call_target="tpu_custom_call" | custom-call | tf_op jit(solution)/shard_map/store/pallas_call | solution.py:675

commit v7 on v6

--- a/solution.py
+++ b/solution.py
@@ -9,7 +9,8 @@
 
 REACH = 2
 CHUNKS = 3
-PARTS = 2
+PARTS = 4
+DIRECT = 3
 STORES = 4
 MESH = pl.DeviceIdType.MESH
 
@@ -33,7 +34,7 @@
         spots = [self.spot(w, max_of=max) for w in range(self.half)]
         self.most = max(max(below, above) for _, below, above in spots)
         assert self.most <= planes and 8 * vectors == width
-        assert spots[0][1] == spots[-1][2] > 4 and spots[0][2] == spots[-1][1] == 0
+        assert spots[0][1] == spots[-1][2] > 3 + DIRECT - 1 and spots[0][2] == spots[-1][1] == 0
         self.end_near = spots[0][1]
         self.most_far = max(min(below, above) for _, below, above in spots)
         self.totals = sorted({count for _, below, above in spots for count in (below, above)} - {0})
@@ -97,10 +98,19 @@
     near_edge = jnp.where(lower, base, base + planes - 1)
     far_edge = jnp.where(lower, base + planes - 1, base)
 
-    load_field = pltpu.make_async_copy(fiedler, field.at[:, pl.ds(base, planes), 0:lines], local_sem.at[0])
-    load_label = pltpu.make_async_copy(labels, label.at[:, 0:lines], local_sem.at[1])
+    chunk = plan.chunk
+    near_start, far_start = jnp.where(lower, 0, planes - chunk), jnp.where(lower, planes - chunk, 0)
+    rest = planes - 2 * chunk
+    loads = []
+    for i, (start, size) in enumerate((
+            (jnp.where(is_end, near_start, far_start), chunk), (jnp.where(is_end, far_start, near_start), chunk),
+            (chunk, rest))):
+        loads.append(pltpu.make_async_copy(
+            fiedler.at[:, pl.ds(start, size)], field.at[:, pl.ds(base + start, size), 0:lines], local_sem.at[i]))
+    load_label = pltpu.make_async_copy(labels, label.at[:, 0:lines], local_sem.at[3])
     load_label.start()
-    load_field.start()
+    for load in loads:
+        load.start()
 
     barrier = pltpu.get_barrier_semaphore()
     def signal(sem, device):
@@ -137,8 +147,6 @@
         remote(label.at[:, lo], label.at[:, nxt], lab_s.at[0], lab_r.at[0], (c, down_l)),
         remote(label.at[:, hi], label.at[:, prv], lab_s.at[0], lab_r.at[0], (c, up_l)),
     ]
-    chunk = plan.chunk
-
     def own_copies(i):
         start = jnp.where(lower, i * chunk, planes - (i + 1) * chunk)
         at = pl.ds(base + start, chunk)
@@ -182,66 +190,82 @@
         ]
 
     def passed_on(j, total):
-        return (j >= 2) & (j <= total - 2)
-
-    def pass_copies(j):
-        at = near_edge + d * j
-        return [
-            remote(field.at[:, at, lo], field.at[:, at, nxt], pass_s.at[0], edge_r.at[j - 1],
-                   (c, down_l)),
-            remote(field.at[:, at, hi], field.at[:, at, prv], pass_s.at[0], edge_r.at[j - 1],
-                   (c, up_l)),
-        ]
-
-    def send_plane(j):
+        return j <= total - DIRECT
+
+    def pass_along(ref, send, recv):
+        remote(ref(lo), ref(nxt), send, recv, (c, down_l)).start()
+        remote(ref(hi), ref(prv), send, recv, (c, up_l)).start()
+
+    def pass_plane(index, at):
+        pass_along(lambda rows: field.at[:, at, rows], pass_s.at[0], edge_r.at[index])
+
+    def send_plane(j, only=(True, True)):
         for way, total, across in sends:
-            @pl.when((j < total) | ((j == total) & jnp.logical_not(across)))
+            @pl.when(((j < total) | ((j == total) & jnp.logical_not(across))) & only[way])
             def _():
                 plane_copy(way, j).start()
 
-            @pl.when((j == total) & across)
+            @pl.when((j == total) & across & only[way])
             def _():
                 for copy in part_copies(way, j):
                     copy.start()
 
     def send_corners(j):
         for way, total, across in sends:
-            @pl.when((j <= total) & jnp.logical_not(across & passed_on(j, total)))
+            target_near = (up_near, down_near)[way]
+
+            direct = jnp.where(target_near, jnp.logical_not(across & passed_on(j, total)), j == total)
+
+            @pl.when((j <= total) & direct)
             def _():
                 for copy in corner_copies(way, j):
                     copy.start()
 
-    def count_copies(way, corners):
-        to = (up_c, down_c)[way]
-        send, recv = cnt_s.at[way], cnt_r.at[count_sem[way]]
-        if not corners:
-            return [remote(count.at[way], counted.at[way, 0:lines], send, recv, (to, l))]
-        return [
-            remote(count.at[way, lo], counted.at[way, nxt], send, recv, (to, down_l)),
-            remote(count.at[way, hi], counted.at[way, prv], send, recv, (to, up_l)),
-        ]
-
-    def start_counts(corners):
+    def start_counts(only):
         for way, total, _ in sends:
-            @pl.when(total > 0)
-            def _():
-                for copy in count_copies(way, corners):
-                    copy.start()
-
+            @pl.when((total > 0) & only[way])
+            def _():
+                remote(count.at[way], counted.at[way, 0:lines], cnt_s.at[way], cnt_r.at[count_sem[way]],
+                       ((up_c, down_c)[way], l)).start()
+
+    def drain(ref, recv):
+        remote(ref, ref, lab_s.at[0], recv, (c, l)).wait_recv()
+
+    def flush(ref, send):
+        remote(ref, ref, send, lab_r.at[0], (c, l)).wait_send()
+
+    both = slice(0, 2 * REACH)
+    incoming = ((near_way, near, 0), (far_way, far, 1))
     partner = c + 1 - 2 * lax.rem(c, 2)
     partner_end = plan.is_end(partner)
     cross_c = lax.rem(c + d + chain, chain)
 
+    def start_chunk(i):
+        for copy in own_copies(i):
+            copy.start()
+
     def start_lanes():
         for copy in lab_copies:
             copy.start()
-        for i in range(CHUNKS):
-            for copy in own_copies(i):
-                copy.start()
-
-    load_field.wait()
-    start_counts(False)
-    send_plane(1)
+        start_chunk(0)
+
+    def pass_counts():
+        for way, total, index in incoming:
+            @pl.when(total > 0)
+            def _():
+                drain(counted.at[way, 0:lines], cnt_r.at[index])
+                pass_along(lambda rows: counted.at[way, rows], cnt_s.at[2 + index], cnt_r.at[2 + index])
+
+    down_first = lower == is_end
+    ahead = min(chunk, most - DIRECT)
+    for load, only in zip(loads, ((jnp.logical_not(down_first), down_first), (down_first, jnp.logical_not(down_first)))):
+        load.wait()
+        start_counts(only)
+        for j in range(1, ahead + 1):
+            send_plane(j, only)
+    loads[2].wait()
+    for j in range(ahead + 1, most - DIRECT + 1):
+        send_plane(j)
 
     @pl.when(is_end)
     def _():
@@ -249,6 +273,8 @@
         signal(cross.at[0], (cross_c, l))
         start_lanes()
         pl.semaphore_wait(cross.at[0], 1)
+        pass_counts()
+        start_chunk(1)
 
     @pl.when(jnp.logical_not(is_end))
     def _():
@@ -261,12 +287,14 @@
 
         signal(lane_told.at[1], (c, up_l))
         signal(lane_told.at[1], (c, down_l))
-
-    start_counts(True)
-    send_corners(1)
-    for j in range(2, most + 1):
-        send_corners(j)
-        send_plane(j)
+        pass_counts()
+        start_chunk(1)
+
+    def send_rest():
+        for j in range(1, most + 1):
+            send_corners(j)
+            if j > most - DIRECT:
+                send_plane(j)
 
     @pl.when(jnp.logical_not(is_end))
     def _():
@@ -289,13 +317,6 @@
 
     tell_chain(0)
 
-    def drain(ref, recv):
-        remote(ref, ref, lab_s.at[0], recv, (c, l)).wait_recv()
-
-    def flush(ref, send):
-        remote(ref, ref, send, lab_r.at[0], (c, l)).wait_send()
-
-    both = slice(0, 2 * REACH)
     drain(label.at[:, both], lab_r.at[0])
     acc[...] = jnp.zeros(acc.shape, jnp.float32)
     for p in range(planes):
@@ -416,18 +437,22 @@
 
         @pl.when(is_end & passed_on(j, near))
         def _():
-            for copy in pass_copies(j):
-                copy.start()
+            pass_plane(j - 1, near_edge + d * j)
+
+    def near_use_now(j):
+        lax.fori_loop(j, j + 1, near_use, 0)
 
     def near_step(j, _):
-        arrive(j)
-        begin = jnp.where(is_end & passed_on(j - 1, near), j - 1, j)
-        lax.fori_loop(begin, jnp.where(is_end & passed_on(j, near), j, j + 1), near_use, 0)
+        wait_plane(j - 1, near_edge + d * j)
+        near_use(j, 0)
         return 0
 
     def far_step(j, _):
         at = far_edge - d * j
-        wait_plane(most + j - 1, at)
+        @pl.when(j == far)
+        def _():
+            wait_plane(most + j - 1, at)
+
         wait_edges(most + j - 1, at)
         mark[at] = jnp.where(counted[far_way] >= (far - j + 1).astype(jnp.float32) - 0.5, 1.0, 0.0)
         take(at)
@@ -473,7 +498,7 @@
     def end_gram():
         @pl.when(is_end)
         def _():
-            lax.fori_loop(1, 2, near_step, 0)
+            near_use_now(1)
             lax.fori_loop(1, near + 1, other_step, 0)
             add_gram([lambda g, p=p: spare[:, p, 8 * g : 8 * g + 8, :] for p in range(plan.end_near)], 1)
 
@@ -481,15 +506,23 @@
     for i in range(CHUNKS):
         drain(field.at[:, 0:chunk, both], own_r.at[i])
         chain_rounds(i)
+        if i == 0:
+            @pl.when(is_end)
+            def _():
+                arrive(1)
+
+            for more in range(2, CHUNKS):
+                start_chunk(more)
+            send_rest()
         lax.fori_loop(i * chunk, (i + 1) * chunk, take_own, 0)
         inner = max(1, i * chunk - 1), (i + 1) * chunk - 1
         lax.fori_loop(*inner, inner_once, 0)
         gram_of([(near_edge - d * m, True) for m in range(*inner)])
         if i == ready:
-            for way, total in ((near_way, near), (far_way, far)):
+            for way, total, index in incoming:
                 @pl.when(total > 0)
                 def _():
-                    drain(counted.at[way, 0 : lines + 2 * REACH], cnt_r.at[0 if way is near_way else 1])
+                    drain(counted.at[way, both], cnt_r.at[2 + index])
             end_gram()
 
             @pl.when(is_end)
@@ -498,6 +531,13 @@
 
     @pl.when(jnp.logical_not(is_end))
     def _():
+        def far_arrive(j, _):
+            at = far_edge - d * j
+            wait_plane(most + j - 1, at)
+            pass_plane(most + j - 1, at)
+            return 0
+
+        lax.fori_loop(1, far, far_arrive, 0)
         lax.fori_loop(1, near + 1, near_step, 0)
         gram_of([(near_edge + d * (j - 1), j <= near) for j in range(1, most + 1)])
 
@@ -553,8 +593,14 @@
 
     @pl.when(is_end)
     def _():
-        lax.fori_loop(2, 3, near_use, 0)
-        lax.fori_loop(4, near, near_step, 0)
+        for j in range(4, plan.end_near - DIRECT + 1):
+            arrive(j)
+        lax.fori_loop(2, near - DIRECT + 1, near_use, 0)
+        lax.fori_loop(near - DIRECT + 1, near, near_step, 0)
+
+    @pl.when(is_end)
+    def _():
+        last_use()
 
     def many(total):
         return remote(got.at[0:total, 0:count_rows], got.at[0:total, 0:count_rows], gram_s.at[0], gram_r.at[0], (c, l))
@@ -599,24 +645,39 @@
 
     @pl.when(is_end)
     def _():
-        flush(field.at[:, 0 : plan.end_near - 3, both], pass_s.at[0])
-        last_use()
+        flush(field.at[:, 0 : plan.end_near - DIRECT, both], pass_s.at[0])
+
+    for index, total in enumerate((near, far)):
+        @pl.when(total > 0)
+        def _():
+            flush(counted.at[0, both], cnt_s.at[2 + index])
+
+    for t in range(1, plan.most_far):
+        @pl.when(far == t + 1)
+        def _():
+            flush(field.at[:, 0:t, both], pass_s.at[0])
 
     for way, total, across in sends:
+        target_near = (up_near, down_near)[way]
+
         @pl.when(total > 0)
         def _():
-            flush(counted.at[way, 0 : lines + 2 * REACH], cnt_s.at[way])
+            flush(counted.at[way, 0:lines], cnt_s.at[way])
 
         @pl.when(across)
         def _():
-            flush(field.at[:, 0:3, both], corner_s.at[way])
+            flush(field.at[:, 0:DIRECT, both], corner_s.at[way])
+
+        @pl.when((total > 0) & jnp.logical_not(target_near))
+        def _():
+            flush(field.at[:, 0:1, both], corner_s.at[way])
 
         for t in plan.totals:
             @pl.when(total == t)
             def _():
                 flush(field.at[:, 0:t, 0:lines], plane_s.at[way])
 
-            @pl.when((total == t) & jnp.logical_not(across))
+            @pl.when((total == t) & target_near & jnp.logical_not(across))
             def _():
                 flush(field.at[:, 0:t, both], corner_s.at[way])
 
@@ -663,9 +724,9 @@
             pltpu.VMEM((8, width), f32),
             pltpu.VMEM((8, width), f32),
             pltpu.VMEM((chain * lanes, 8, width), f32),
-            dma((2,)), dma((1,)), dma((1,)), dma((1,)), dma((CHUNKS,)),
+            dma((4,)), dma((1,)), dma((1,)), dma((1,)), dma((CHUNKS,)),
             dma((2,)), dma((most + plan.most_far,)), dma((PARTS,)), dma((2,)), dma((most + plan.most_far,)),
-            dma((1,)), dma((2,)), dma((2,)), dma((1,)), dma((1,)), dma((1,)), dma((1,)),
+            dma((1,)), dma((4,)), dma((4,)), dma((1,)), dma((1,)), dma((1,)), dma((1,)),
             regular((lanes // 2,)), regular((1,)), regular((1,)), regular((plan.rounds,)),
         ],
         compiler_params=pltpu.CompilerParams(

time: 35.4 us -> 33.8 us (0.955)
  Pallas kernels: 34.7 us -> 33 us
    pallas_call x1, Pallas kernels: 32.7 us -> 31 us  [per_device(): pl.pallas_call(functools.partial(kernel, plan, float(slots)), in_specs=[a...]
where the time goes in v7:
time: 33.8 us; the launch traced here: 33.6 us
  Pallas kernels  33 us (98%)
  between operations  0.64 us (2%)
    pallas_call x1, Pallas kernels, per_device(): pl.pallas_call(functools.partial(kernel, plan, float(slots)), in_specs=[a...  31 us
    pallas_call x1, Pallas kernels, per_device(): pl.pallas_call(store_kernel, in_specs=[vmem, vmem], out_specs=[anywhere,...  1.97 us

profile of v7, /device:TPU:1, one launch (start us, length us, event | category | flops | bytes accessed | tf_op | source)
XLA Modules:
  0.0 33.6 jit_solution(3136285092478401661)
XLA Ops:
  0.6 31.0 %laplace.1 = (f32[16,15,32,128]{3,2,1,0:T(8,128)S(1)}, f32[2,16,16]{2,1,0:T(8,128)S(1)}) custom-call(f32[16,12,32,128]{3,2,1,0:T(8,128)} %fiedler.1, s32[12,32,128]{2,1,0:T(8,128)} %labels.1), custom_call_target="tpu_custom_call" | custom-call | tf_op jit(solution)/shard_map/laplace/pallas_call | solution.py:705
  31.6 2.0 %store.1 = (f32[16,15,32,128]{3,2,1,0:T(8,128)}, f32[2,16,16]{2,1,0:T(8,128)}) custom-call(f32[16,15,32,128]{3,2,1,0:T(8,128)S(1)} %get-tuple-element.4.image, f32[2,16,16]{2,1,0:T(8,128)S(1)} %get-tuple-element.5.gram), custom_call_target="tpu_custom_call" | custom-call | tf_op jit(solution)/shard_map/store/pallas_call | solution.py:736

commit v8 on v7

--- a/solution.py
+++ b/solution.py
@@ -11,6 +11,7 @@
 CHUNKS = 3
 PARTS = 4
 DIRECT = 3
+EARLY = 4
 STORES = 4
 MESH = pl.DeviceIdType.MESH
 
@@ -33,7 +34,7 @@
         self.window = self.band + 2 * REACH
         spots = [self.spot(w, max_of=max) for w in range(self.half)]
         self.most = max(max(below, above) for _, below, above in spots)
-        assert self.most <= planes and 8 * vectors == width
+        assert self.most <= planes and 8 * vectors == width and spots[0][1] == self.most
         assert spots[0][1] == spots[-1][2] > 3 + DIRECT - 1 and spots[0][2] == spots[-1][1] == 0
         self.end_near = spots[0][1]
         self.most_far = max(min(below, above) for _, below, above in spots)
@@ -257,14 +258,14 @@
                 pass_along(lambda rows: counted.at[way, rows], cnt_s.at[2 + index], cnt_r.at[2 + index])
 
     down_first = lower == is_end
-    ahead = min(chunk, most - DIRECT)
+    ahead = min(chunk, EARLY)
     for load, only in zip(loads, ((jnp.logical_not(down_first), down_first), (down_first, jnp.logical_not(down_first)))):
         load.wait()
         start_counts(only)
         for j in range(1, ahead + 1):
             send_plane(j, only)
     loads[2].wait()
-    for j in range(ahead + 1, most - DIRECT + 1):
+    for j in range(ahead + 1, EARLY + 1):
         send_plane(j)
 
     @pl.when(is_end)
@@ -293,7 +294,7 @@
     def send_rest():
         for j in range(1, most + 1):
             send_corners(j)
-            if j > most - DIRECT:
+            if j > EARLY:
                 send_plane(j)
 
     @pl.when(jnp.logical_not(is_end))
@@ -403,7 +404,7 @@
         apply_twice(at - 2 * d)
         return 0
 
-    def last_use():
+    def last_use(before_last):
         at = near_edge + d * near
         near_mark(near)
         for i in range(3):
@@ -429,6 +430,8 @@
 
         share = vectors // PARTS
         for i in range(PARTS):
+            if i == PARTS - 1:
+                before_last()
             drain(field.at[i * share : (i + 1) * share, at, 0:lines], last_r.at[i])
             lax.fori_loop(i * share, (i + 1) * share, one, 0, unroll=share)
 
@@ -598,38 +601,78 @@
         lax.fori_loop(2, near - DIRECT + 1, near_use, 0)
         lax.fori_loop(near - DIRECT + 1, near, near_step, 0)
 
-    @pl.when(is_end)
-    def _():
-        last_use()
-
     def many(total):
         return remote(got.at[0:total, 0:count_rows], got.at[0:total, 0:count_rows], gram_s.at[0], gram_r.at[0], (c, l))
 
-    @pl.when(leads)
-    def _():
-        many(chips - 1).wait_recv()
-
-    @pl.when(jnp.logical_not(leads))
-    def _():
-        chain_rounds(3)
-        many(chips).wait_recv()
-
-    def sum_one(i, total):
-        return total + got[i, 0:count_rows]
-
-    total = lax.fori_loop(1, chips, sum_one, got[0, 0:count_rows], unroll=True)
-    tall_shape = (vectors, width)
-    inside = lax.div(lane_of(tall_shape, 1), 8) == lane_of(tall_shape, 0)
-    choose = jnp.where(
-        lax.rem(lane_of((width, width), 0), 8) == lax.rem(lane_of((width, width), 1), 8), 1.0, 0.0)
-    for place in range(2):
-        result = jnp.zeros(tall_shape, jnp.float32)
-        for h in range(vectors // 8):
-            i = place * (vectors // 8) + h
-            spread = jnp.where(inside, jnp.broadcast_to(total[i : i + 1], tall_shape), 0.0)
-            spread = jnp.dot(spread, choose, precision=lax.Precision.HIGHEST, preferred_element_type=jnp.float32)
-            result = jnp.where(lax.div(lane_of(tall_shape, 1), 8) == h, spread, result)
-        gram[place] = result[:, 0:vectors] / scale_of
+    def finish_gram():
+        @pl.when(leads)
+        def _():
+            many(chips - 1).wait_recv()
+
+        @pl.when(jnp.logical_not(leads))
+        def _():
+            chain_rounds(3)
+            many(chips).wait_recv()
+
+        def sum_one(i, total):
+            return total + got[i, 0:count_rows]
+
+        total = lax.fori_loop(1, chips, sum_one, got[0, 0:count_rows], unroll=True)
+        tall_shape = (vectors, width)
+        inside = lax.div(lane_of(tall_shape, 1), 8) == lane_of(tall_shape, 0)
+        choose = jnp.where(
+            lax.rem(lane_of((width, width), 0), 8) == lax.rem(lane_of((width, width), 1), 8), 1.0, 0.0)
+        for place in range(2):
+            result = jnp.zeros(tall_shape, jnp.float32)
+            for h in range(vectors // 8):
+                i = place * (vectors // 8) + h
+                spread = jnp.where(inside, jnp.broadcast_to(total[i : i + 1], tall_shape), 0.0)
+                spread = jnp.dot(spread, choose, precision=lax.Precision.HIGHEST, preferred_element_type=jnp.float32)
+                result = jnp.where(lax.div(lane_of(tall_shape, 1), 8) == h, spread, result)
+            gram[place] = result[:, 0:vectors] / scale_of
+
+    def flush_early():
+        flush(field.at[:, 0:planes, both], own_s.at[0])
+        flush(label.at[:, both], lab_s.at[0])
+        for index, total in enumerate((near, far)):
+            @pl.when(total > 0)
+            def _():
+                flush(counted.at[0, both], cnt_s.at[2 + index])
+
+        for t in range(1, plan.most_far):
+            @pl.when(far == t + 1)
+            def _():
+                flush(field.at[:, 0:t, both], pass_s.at[0])
+
+        for way, total, across in sends:
+            target_near = (up_near, down_near)[way]
+
+            @pl.when(total > 0)
+            def _():
+                flush(counted.at[way, 0:lines], cnt_s.at[way])
+
+            @pl.when((total > 0) & jnp.logical_not(target_near))
+            def _():
+                flush(field.at[:, 0:1, both], corner_s.at[way])
+
+            for t in plan.totals:
+                @pl.when((total == t) & jnp.logical_not(across))
+                def _():
+                    flush(field.at[:, 0:t, 0:lines], plane_s.at[way])
+
+                @pl.when((total == t) & target_near & jnp.logical_not(across))
+                def _():
+                    flush(field.at[:, 0:t, both], corner_s.at[way])
+
+    @pl.when(is_end)
+    def _():
+        flush(field.at[:, 0 : plan.end_near - DIRECT, both], pass_s.at[0])
+        flush_early()
+        last_use(finish_gram)
+
+    @pl.when(jnp.logical_not(is_end))
+    def _():
+        finish_gram()
 
     @pl.when(leads)
     def _():
@@ -640,46 +683,15 @@
     def _():
         hand_over.wait_send()
 
-    flush(field.at[:, 0:planes, both], own_s.at[0])
-    flush(label.at[:, both], lab_s.at[0])
-
-    @pl.when(is_end)
-    def _():
-        flush(field.at[:, 0 : plan.end_near - DIRECT, both], pass_s.at[0])
-
-    for index, total in enumerate((near, far)):
-        @pl.when(total > 0)
-        def _():
-            flush(counted.at[0, both], cnt_s.at[2 + index])
-
-    for t in range(1, plan.most_far):
-        @pl.when(far == t + 1)
-        def _():
-            flush(field.at[:, 0:t, both], pass_s.at[0])
-
-    for way, total, across in sends:
-        target_near = (up_near, down_near)[way]
-
-        @pl.when(total > 0)
-        def _():
-            flush(counted.at[way, 0:lines], cnt_s.at[way])
-
+    @pl.when(jnp.logical_not(is_end))
+    def _():
+        flush_early()
+
+    for way, _, across in sends:
         @pl.when(across)
         def _():
+            flush(field.at[:, 0:most, 0:lines], plane_s.at[way])
             flush(field.at[:, 0:DIRECT, both], corner_s.at[way])
-
-        @pl.when((total > 0) & jnp.logical_not(target_near))
-        def _():
-            flush(field.at[:, 0:1, both], corner_s.at[way])
-
-        for t in plan.totals:
-            @pl.when(total == t)
-            def _():
-                flush(field.at[:, 0:t, 0:lines], plane_s.at[way])
-
-            @pl.when((total == t) & target_near & jnp.logical_not(across))
-            def _():
-                flush(field.at[:, 0:t, both], corner_s.at[way])
 
 
 def store_kernel(image, gram, image_out, gram_out, sems):

time: 33.8 us -> 33.5 us (level)
  no operation moved by 1% of the time
where the time goes in v8:
time: 33.5 us; the launch traced here: 33.3 us
  Pallas kernels  32.7 us (98%)
  between operations  0.64 us (2%)
    pallas_call x1, Pallas kernels, per_device(): pl.pallas_call(functools.partial(kernel, plan, float(slots)), in_specs=[a...  30.7 us
    pallas_call x1, Pallas kernels, per_device(): pl.pallas_call(store_kernel, in_specs=[vmem, vmem], out_specs=[anywhere,...  1.97 us

profile of v8, /device:TPU:1, one launch (start us, length us, event | category | flops | bytes accessed | tf_op | source)
XLA Modules:
  0.0 33.3 jit_solution(8810026816062934182)
XLA Ops:
  0.6 30.7 %laplace.1 = (f32[16,15,32,128]{3,2,1,0:T(8,128)S(1)}, f32[2,16,16]{2,1,0:T(8,128)S(1)}) custom-call(f32[16,12,32,128]{3,2,1,0:T(8,128)} %fiedler.1, s32[12,32,128]{2,1,0:T(8,128)} %labels.1), custom_call_target="tpu_custom_call" | custom-call | tf_op jit(solution)/shard_map/laplace/pallas_call | solution.py:717
  31.4 2.0 %store.1 = (f32[16,15,32,128]{3,2,1,0:T(8,128)}, f32[2,16,16]{2,1,0:T(8,128)}) custom-call(f32[16,15,32,128]{3,2,1,0:T(8,128)S(1)} %get-tuple-element.4.image, f32[2,16,16]{2,1,0:T(8,128)S(1)} %get-tuple-element.5.gram), custom_call_target="tpu_custom_call" | custom-call | tf_op jit(solution)/shard_map/store/pallas_call | solution.py:748

commit v9 on v8

--- a/solution.py
+++ b/solution.py
@@ -109,8 +109,7 @@
         loads.append(pltpu.make_async_copy(
             fiedler.at[:, pl.ds(start, size)], field.at[:, pl.ds(base + start, size), 0:lines], local_sem.at[i]))
     load_label = pltpu.make_async_copy(labels, label.at[:, 0:lines], local_sem.at[3])
-    load_label.start()
-    for load in loads:
+    for load in (loads[0], load_label, loads[1], loads[2]):
         load.start()
 
     barrier = pltpu.get_barrier_semaphore()

time: 33.5 us -> 33.5 us (level)
  no operation moved by 1% of the time
where the time goes in v9:
time: 33.5 us; the launch traced here: 33.4 us
  Pallas kernels  32.7 us (98%)
  between operations  0.64 us (2%)
    pallas_call x1, Pallas kernels, per_device(): pl.pallas_call(functools.partial(kernel, plan, float(slots)), in_specs=[a...  30.8 us
    pallas_call x1, Pallas kernels, per_device(): pl.pallas_call(store_kernel, in_specs=[vmem, vmem], out_specs=[anywhere,...  1.97 us

profile of v9, /device:TPU:1, one launch (start us, length us, event | category | flops | bytes accessed | tf_op | source)
XLA Modules:
  0.0 33.4 jit_solution(13440576652406611332)
XLA Ops:
  0.6 30.8 %laplace.1 = (f32[16,15,32,128]{3,2,1,0:T(8,128)S(1)}, f32[2,16,16]{2,1,0:T(8,128)S(1)}) custom-call(f32[16,12,32,128]{3,2,1,0:T(8,128)} %fiedler.1, s32[12,32,128]{2,1,0:T(8,128)} %labels.1), custom_call_target="tpu_custom_call" | custom-call | tf_op jit(solution)/shard_map/laplace/pallas_call | solution.py:716
  31.4 2.0 %store.1 = (f32[16,15,32,128]{3,2,1,0:T(8,128)}, f32[2,16,16]{2,1,0:T(8,128)}) custom-call(f32[16,15,32,128]{3,2,1,0:T(8,128)S(1)} %get-tuple-element.4.image, f32[2,16,16]{2,1,0:T(8,128)S(1)} %get-tuple-element.5.gram), custom_call_target="tpu_custom_call" | custom-call | tf_op jit(solution)/shard_map/store/pallas_call | solution.py:747
